TPU v7x, 32 devices: a whole 2x2x4 slice. The times are simulated.
32 devices in a mesh: gx: 4 (over x, core), gy: 4 (over z), gz: 2 (over y).
Axes of the slice: x: 2, y: 2, z: 4, core: 2. Of those that a mesh axis runs over, the one named last changes fastest.
Arguments:
- occupied: float32 [16, 16, 16, 256], P(None, 'gx', 'gy', 'gz'), may hold values from -6 to 6
- virtual: float32 [16, 16, 16, 256], P(None, 'gx', 'gy', 'gz'), may hold values from -6 to 6
- kernel_fields: float32 [4, 16, 16, 256], P(None, 'gx', 'gy', 'gz'), may hold values from -1.5 to 1.5
- density_grad: float32 [3, 16, 16, 256], P(None, 'gx', 'gy', 'gz'), may hold values from -6 to 6
Outputs:
- potential: float32 [256, 16, 16, 256], P(None, 'gx', 'gy', 'gz')
- casida: float32 [256, 256], P(('gx', 'gy', 'gz'))
All inputs are finite; a program needn't handle non-finite values.
Results may differ from a plain program's by a relative error of at most 0.00013.
Values sent between devices are 32-bit elements; how exact they have to be, the bound alone decides.
A program may use at most 64 MiB of HBM per device.

v0:
```python
import jax
import jax.numpy as jnp
from jax import lax
from jax.sharding import PartitionSpec as P


def padded(block, sides, width):
    for axis, dim in sides:
        count = lax.axis_size(axis)
        forward = [(i, i + 1) for i in range(count - 1)]
        forward.append((count - 1, 0))
        backward = [(target, source) for source, target in forward]
        low = lax.ppermute(
            lax.slice_in_dim(block, block.shape[dim] - width, None, axis=dim), axis, forward
        )
        high = lax.ppermute(lax.slice_in_dim(block, 0, width, axis=dim), axis, backward)
        block = jnp.concatenate([low, block, high], axis=dim)
    return block


def window(values, offsets):
    starts = (0,) + tuple((2 + offsets[dimension] for dimension in range(3)))
    limits = (values.shape[0],) + tuple(
        (values.shape[dimension + 1] - 2 + offsets[dimension] for dimension in range(3))
    )
    return lax.slice(values, starts, limits)


def derivative(values, dimension):

    def shifted(offset):
        offsets = [0, 0, 0]
        offsets[dimension] = offset
        return window(values, offsets)

    inner_diff = shifted(1) - shifted(-1)
    outer_diff = shifted(2) - shifted(-2)
    return (8.0 * inner_diff - outer_diff) / 12.0


def trim_rim(values, margin):
    return values[:, margin:-margin, margin:-margin, margin:-margin]


def on_device(occupied, virtual, kernel_fields, density_grad):
    local_kernel = kernel_fields[0]
    mixed_kernel = kernel_fields[1]
    nvir = virtual.shape[0]
    occ_wide = padded(occupied, (("gx", 1), ("gy", 2), ("gz", 3)), 4)
    vir_wide = padded(virtual, (("gx", 1), ("gy", 2), ("gz", 3)), 4)
    stacked = jnp.concatenate([kernel_fields, density_grad], axis=0)
    field_wide = padded(stacked, (("gx", 1), ("gy", 2), ("gz", 3)), 2)

    def pair_block(scan_state, orbital):
        dens_wide = orbital[None] * vir_wide
        slopes = [derivative(dens_wide, dimension) for dimension in range(3)]
        dens_middle = trim_rim(dens_wide, 2)
        aligned = field_wide[4] * slopes[0] + field_wide[5] * slopes[1] + field_wide[6] * slopes[2]
        scalar = field_wide[1] * dens_middle + field_wide[2] * aligned
        fluxes = [
            scalar * field_wide[4 + dimension] + field_wide[3] * slopes[dimension]
            for dimension in range(3)
        ]
        divergence = derivative(fluxes[0], 0) + derivative(fluxes[1], 1) + derivative(fluxes[2], 2)
        return (
            scan_state,
            local_kernel * trim_rim(dens_middle, 2)
            + mixed_kernel * trim_rim(aligned, 2)
            - divergence,
        )

    unused_state, stacked_potential = lax.scan(pair_block, jnp.zeros((), jnp.float32), occ_wide)
    nocc = occupied.shape[0]
    cells = occupied.shape[1] * occupied.shape[2] * occupied.shape[3]
    potential = stacked_potential.reshape((nocc * nvir,) + occupied.shape[1:])
    devices_all = lax.axis_size("gx") * lax.axis_size("gy") * lax.axis_size("gz")
    total_cells = cells * devices_all
    flat_potential = potential.reshape((nocc * nvir, cells))
    occ_flat = occupied.reshape((nocc, cells))
    vir_flat = virtual.reshape((nvir, cells))
    own_rows = nocc * nvir // devices_all
    pair_index = lax.iota(jnp.int32, lax.axis_size(("gx", "gy", "gz")) * own_rows)
    occ_pick = (pair_index[:, None] // nvir == lax.iota(jnp.int32, nocc)[None, :]).astype(
        jnp.float32
    )
    vir_pick = (pair_index[:, None] % nvir == lax.iota(jnp.int32, nvir)[None, :]).astype(
        jnp.float32
    )
    occ_rows = jnp.dot(
        occ_pick, occ_flat, precision=lax.Precision.HIGHEST, preferred_element_type=jnp.float32
    )
    vir_rows = jnp.dot(
        vir_pick, vir_flat, precision=lax.Precision.HIGHEST, preferred_element_type=jnp.float32
    )
    casida = lax.psum_scatter(
        lax.dot_general(
            occ_rows * vir_rows,
            flat_potential,
            (((1,), (1,)), ((), ())),
            precision=lax.Precision.HIGHEST,
            preferred_element_type=jnp.float32,
        ),
        ("gx", "gy", "gz"),
        scatter_dimension=0,
        tiled=True,
    ) * (1.0 / total_cells)
    return (potential, casida)


def solution(mesh):
    placed = (
        P(None, "gx", "gy", "gz"),
        P(None, "gx", "gy", "gz"),
        P(None, "gx", "gy", "gz"),
        P(None, "gx", "gy", "gz"),
    )
    return jax.shard_map(
        on_device,
        mesh=mesh,
        in_specs=placed,
        out_specs=(P(None, "gx", "gy", "gz"), P(("gx", "gy", "gz"), None)),
        check_vma=False,
    )
```

profile of v0, /device:TPU:0, one launch (start us, length us, event | category | flops | bytes accessed | tf_op | source)
XLA Modules:
  0.0 404.4 jit_solution(8782214869207041111)
XLA Ops:
  7.2 1.6 copy.21
  9.3 1.9 collective-permute-start.7
  14.6 1.6 copy.14
  19.0 1.8 collective-permute-start.14
  20.8 2.1 collective-permute-start.15
  22.9 2.3 convolution_multiply_fusion
  26.8 1.4 collective-permute-start.16
  28.9 6.4 %collective-permute-done.16 = f32[7,8,8,2]{3,2,1,0:T(8,128)S(1)} collective-permute-done((f32[7,8,8,2]{3,2,1,0:T(8,128)S(1)}, f32[7,8,8,2]{3,2,1,0:T(8,128)S(1)}, u32[]{:S(2)}, u32[]{:S(2)}) %collective-permute-start.16) | collective-permute-done | bytes 3616 | tf_op jit(solution)/shard_map/ppermute | solution.py:13
  35.4 4.1 %collective-permute-done.17 = f32[7,8,8,2]{3,2,1,0:T(8,128)S(1)} collective-permute-done((f32[7,8,8,2]{3,2,1,0:T(8,128)S(1)}, f32[7,8,8,2]{3,2,1,0:T(8,128)S(1)}, u32[]{:S(2)}, u32[]{:S(2)}) %collective-permute-start.17) | collective-permute-done | bytes 3616 | tf_op jit(solution)/shard_map/ppermute | solution.py:16
  43.7 2.8 collective-permute-start.9
  47.6 3.8 collective-permute-start.3
  51.4 5.1 %collective-permute-done.8 = f32[16,12,4,128]{3,0,2,1:T(8,128)S(1)} collective-permute-done((f32[16,12,4,128]{3,0,2,1:T(8,128)S(1)}, f32[16,12,4,128]{3,0,2,1:T(8,128)S(1)}, u32[]{:S(2)}, u32[]{:S(2)}) %collective-permute-start.8) | collective-permute-done | bytes 393248 | tf_op jit(solution)/shard_map/ppermute | solution.py:13
  56.4 8.5 %collective-permute-done.9 = f32[16,12,4,128]{3,0,2,1:T(8,128)S(1)} collective-permute-done((f32[16,12,4,128]{3,0,2,1:T(8,128)S(1)}, f32[16,12,4,128]{3,0,2,1:T(8,128)S(1)}, u32[]{:S(2)}, u32[]{:S(2)}) %collective-permute-start.9) | collective-permute-done | bytes 393248 | tf_op jit(solution)/shard_map/ppermute | solution.py:16
  66.2 1.6 copy.33
  67.8 1.4 collective-permute-start.10
  69.2 1.6 copy.34
  71.5 2.0 collective-permute-done.2
  73.4 5.6 %collective-permute-done.3 = f32[16,12,4,128]{3,0,2,1:T(8,128)} collective-permute-done((f32[16,12,4,128]{3,0,2,1:T(8,128)S(1)}, f32[16,12,4,128]{3,0,2,1:T(8,128)}, u32[]{:S(2)}, u32[]{:S(2)}) %collective-permute-start.3) | collective-permute-done | bytes 393248 | tf_op jit(solution)/shard_map/ppermute | solution.py:16
  80.6 1.7 copy.31
  82.3 1.5 collective-permute-start.4
  83.8 1.6 copy.32
  85.9 1.9 copy.26
  87.8 1.9 copy.27
  89.7 2.0 pad_maximum_fusion.1
  91.7 1.4 copy.29
  93.1 2.9 copy.19
  96.8 2.9 copy.20
  99.7 4.3 %pad_maximum_fusion = f32[16,12,12,136]{3,0,2,1:T(8,128)} fusion(f32[16,12,12,4]{3,0,2,1:T(8,128)} %copy.20, f32[16,12,4,128]{3,0,2,1:T(8,128)} %collective-permute-done.3, f32[16,12,4,128]{3,0,2,1:T(8,128)S(1)} %constant_dynamic-update-slice_fusion, f32[16,12,4,128]{3,0,2,1:T(8,128)} %collective-permute-done.2, f32[16,12,12,4]{3,0,2,1:T(8,128)} %copy.19), kind=kLoop, calls=%fused_computation.52 | loop fusion | flops 1253376 | bytes 2506752 | tf_op jit(solution)/shard_map/concatenate | solution.py:17
  104.0 150.3 %while.10 = (s32[]{:T(128)}, f32[16,16,4,4,128]{4,3,2,1,0:T(4,128)}, f32[1,4,4,128]{3,2,1,0:T(4,128)S(1)}, f32[16,12,12,136]{3,0,2,1:T(8,128)}, f32[16,12,12,136...) while((s32[]{:T(128)}, f32[16,16,4,4,128]{4,3,2,1,0:T(4,128)}, ...), condition=%wide.region_1.2_spmd, body=%wide.region_0.1_spmd.sunk | while | flops 5295106 | bytes 18330712 | solution.py:72
  107.8 3.4 multiply_add_fusion.7
  111.7 1.6 fusion.39
  117.2 3.4 multiply_add_fusion.7
  121.1 1.6 fusion.39
  126.6 3.4 multiply_add_fusion.7
  130.5 1.6 fusion.39
  136.0 3.4 multiply_add_fusion.7
  139.9 1.6 fusion.39
  145.4 3.4 multiply_add_fusion.7
  149.3 1.6 fusion.39
  154.8 3.4 multiply_add_fusion.7
  158.7 1.6 fusion.39
  164.1 3.4 multiply_add_fusion.7
  168.1 1.6 fusion.39
  173.5 3.4 multiply_add_fusion.7
  177.5 1.6 fusion.39
  182.9 3.4 multiply_add_fusion.7
  186.9 1.6 fusion.39
  192.3 3.4 multiply_add_fusion.7
  196.3 1.6 fusion.39
  201.7 3.4 multiply_add_fusion.7
  205.7 1.6 fusion.39
  211.1 3.4 multiply_add_fusion.7
  215.1 1.6 fusion.39
  220.5 3.4 multiply_add_fusion.7
  224.5 1.6 fusion.39
  229.9 3.4 multiply_add_fusion.7
  233.8 1.6 fusion.39
  239.3 3.4 multiply_add_fusion.7
  243.2 1.6 fusion.39
  248.7 3.4 multiply_add_fusion.7
  252.6 1.6 fusion.39
  254.3 3.2 reshape_reshape.3
  257.5 4.2 %fusion.33 = f32[256,256]{1,0:T(8,128)} fusion(f32[256,2048]{1,0:T(8,128)S(1)} %copy-done, f32[256,2048]{1,0:T(8,128)} %reshape_reshape.3), kind=kOutput, calls=%fused_computation.86 | convolution fusion | flops 1610612736 | bytes 4456448 | tf_op jit(solution)/shard_map/dot_general | solution.py:96
  261.7 134.5 %reduce-scatter.2.cloned.1.call-done = f32[8,256]{1,0:T(8,128)} async-done(((f32[256,256]{1,0:T(8,128)}), f32[8,256]{1,0:T(8,128)}) %reduce-scatter.2.cloned.1.call-update) | async-done | bytes 8208 | tf_op jit(solution)/shard_map/reduce_scatter | solution.py:95
  (156 shorter events, 88.6 us)
Async XLA Ops:
  7.2 11.7 %copy-start.2 = (f32[16,4,4,128]{3,2,1,0:T(4,128)S(1)}, f32[16,4,4,128]{3,2,1,0:T(4,128)}, u32[]{:S(2)}) copy-start(f32[16,4,4,128]{3,2,1,0:T(4,128)} %param.7) | copy-start | bytes 393220
  7.2 389.0 %reduce-scatter.2.cloned.1.call-start = ((), (), s32[]{:S(2)}) async-start(), calls=%async_computation.1 | async-start | bytes 270336 | tf_op jit(solution)/shard_map/reduce_scatter | solution.py:95
  8.8 31.9 %collective-permute-start.6 = (f32[16,4,4,128]{3,0,2,1:T(8,128)}, f32[16,4,4,128]{3,0,2,1:T(8,128)}, u32[]{:S(2)}, u32[]{:S(2)}) collective-permute-start(f32[16,4,4,128]{3,0,2,1:T(8,128)} %copy.21), channel_id=1, source_target_pairs={{0,8},{8,16},{16,24},{24,0},{1,9},{9,17},{17,25},{25,1},{2,10},{10... | collective-permute-start | bytes 393224 | tf_op jit(solution)/shard_map/ppermute | solution.py:13
  9.3 32.3 %collective-permute-start.7 = (f32[16,4,4,128]{3,0,2,1:T(8,128)}, f32[16,4,4,128]{3,0,2,1:T(8,128)}, u32[]{:S(2)}, u32[]{:S(2)}) collective-permute-start(f32[16,4,4,128]{3,0,2,1:T(8,128)} %copy.21), channel_id=1, source_target_pairs={{8,0},{16,8},{24,16},{0,24},{9,1},{17,9},{25,17},{1,25},{10,2},{18... | collective-permute-start | bytes 393224 | tf_op jit(solution)/shard_map/ppermute | solution.py:16
  12.8 6.2 %collective-permute-start.12 = (f32[7,2,4,128]{3,2,1,0:T(4,128)S(1)}, f32[7,2,4,128]{3,2,1,0:T(4,128)S(1)}, u32[]{:S(2)}, u32[]{:S(2)}) collective-permute-start(f32[7,2,4,128]{3,2,1,0:T(4,128)S(1)} %get-tuple-element.91), channel_id=1, source_target_pairs={{0,8},{8,16},{16,24},{24,0},{1,9},{9,17},{17,25},{25,1},{2,10},{10... | collective-permute-start | bytes 86024 | tf_op jit(solution)/shard_map/ppermute | solution.py:13
  13.5 5.4 %collective-permute-start.13 = (f32[7,2,4,128]{3,2,1,0:T(4,128)S(1)}, f32[7,2,4,128]{3,2,1,0:T(4,128)S(1)}, u32[]{:S(2)}, u32[]{:S(2)}) collective-permute-start(f32[7,2,4,128]{3,2,1,0:T(4,128)S(1)} %get-tuple-element.92), channel_id=1, source_target_pairs={{8,0},{16,8},{24,16},{0,24},{9,1},{17,9},{25,17},{1,25},{10,2},{18... | collective-permute-start | bytes 86024 | tf_op jit(solution)/shard_map/ppermute | solution.py:16
  16.2 30.3 %collective-permute-start = (f32[16,4,4,128]{3,0,2,1:T(8,128)}, f32[16,4,4,128]{3,0,2,1:T(8,128)}, u32[]{:S(2)}, u32[]{:S(2)}) collective-permute-start(f32[16,4,4,128]{3,0,2,1:T(8,128)} %copy.14), channel_id=1, source_target_pairs={{0,8},{8,16},{16,24},{24,0},{1,9},{9,17},{17,25},{25,1},{2,10},{10... | collective-permute-start | bytes 393224 | tf_op jit(solution)/shard_map/ppermute | solution.py:13
  19.0 6.2 %collective-permute-start.14 = (f32[7,8,2,128]{3,2,1,0:T(2,128)S(1)}, f32[7,8,2,128]{3,2,1,0:T(2,128)S(1)}, u32[]{:S(2)}, u32[]{:S(2)}) collective-permute-start(f32[7,8,2,128]{3,2,1,0:T(2,128)S(1)} %get-tuple-element.89), channel_id=1, source_target_pairs={{0,2},{2,4},{4,6},{6,0},{1,3},{3,5},{5,7},{7,1},{8,10},{10,12},{12... | collective-permute-start | bytes 172040 | tf_op jit(solution)/shard_map/ppermute | solution.py:13
  20.8 8.1 %copy-start.4 = (f32[4,4,4,128]{3,2,1,0:T(4,128)S(1)}, f32[4,4,4,128]{3,2,1,0:T(4,128)}, u32[]{:S(2)}) copy-start(f32[4,4,4,128]{3,2,1,0:T(4,128)} %param.8) | copy-start | bytes 98308
  20.8 5.8 %collective-permute-start.15 = (f32[7,8,2,128]{3,2,1,0:T(2,128)S(1)}, f32[7,8,2,128]{3,2,1,0:T(2,128)S(1)}, u32[]{:S(2)}, u32[]{:S(2)}) collective-permute-start(f32[7,8,2,128]{3,2,1,0:T(2,128)S(1)} %get-tuple-element.90), channel_id=1, source_target_pairs={{2,0},{4,2},{6,4},{0,6},{3,1},{5,3},{7,5},{1,7},{10,8},{12,10},{14... | collective-permute-start | bytes 172040 | tf_op jit(solution)/shard_map/ppermute | solution.py:16
  25.2 22.2 %copy-start.3 = (f32[16,4,4,128]{3,2,1,0:T(4,128)S(1)}, f32[16,4,4,128]{3,2,1,0:T(4,128)}, u32[]{:S(2)}) copy-start(f32[16,4,4,128]{3,2,1,0:T(4,128)} %param.6) | copy-start | bytes 393220
  26.8 8.5 %collective-permute-start.16 = (f32[7,8,8,2]{3,2,1,0:T(8,128)S(1)}, f32[7,8,8,2]{3,2,1,0:T(8,128)S(1)}, u32[]{:S(2)}, u32[]{:S(2)}) collective-permute-start(f32[7,8,8,2]{3,2,1,0:T(8,128)S(1)} %get-tuple-element.87), channel_id=1, source_target_pairs={{0,1},{1,0},{2,3},{3,2},{4,5},{5,4},{6,7},{7,6},{8,9},{9,8},{10,11... | collective-permute-start | bytes 10760 | tf_op jit(solution)/shard_map/ppermute | solution.py:13
  28.3 11.2 %collective-permute-start.17 = (f32[7,8,8,2]{3,2,1,0:T(8,128)S(1)}, f32[7,8,8,2]{3,2,1,0:T(8,128)S(1)}, u32[]{:S(2)}, u32[]{:S(2)}) collective-permute-start(f32[7,8,8,2]{3,2,1,0:T(8,128)S(1)} %get-tuple-element.88), channel_id=1, source_target_pairs={{1,0},{0,1},{3,2},{2,3},{5,4},{4,5},{7,6},{6,7},{9,8},{8,9},{11,10... | collective-permute-start | bytes 10760 | tf_op jit(solution)/shard_map/ppermute | solution.py:16
  35.4 12.1 %collective-permute-start.1 = (f32[16,4,4,128]{3,0,2,1:T(8,128)}, f32[16,4,4,128]{3,0,2,1:T(8,128)S(1)}, u32[]{:S(2)}, u32[]{:S(2)}) collective-permute-start(f32[16,4,4,128]{3,0,2,1:T(8,128)} %copy.14), channel_id=1, source_target_pairs={{8,0},{16,8},{24,16},{0,24},{9,1},{17,9},{25,17},{1,25},{10,2},{18... | collective-permute-start | bytes 393224 | tf_op jit(solution)/shard_map/ppermute | solution.py:16
  42.6 13.8 %collective-permute-start.8 = (f32[16,12,4,128]{3,0,2,1:T(8,128)S(1)}, f32[16,12,4,128]{3,0,2,1:T(8,128)S(1)}, u32[]{:S(2)}, u32[]{:S(2)}) collective-permute-start(f32[16,12,4,128]{3,0,2,1:T(8,128)S(1)} %constant_dynamic-update-slice_fusion.3), channel_id=1, source_target_pairs={{0,2},{2,4},{4,6},{6,0},{1,3},{3,5},{5,7},{7,1},{8,10},{10,12},{12... | collective-permute-start | bytes 1179656 | tf_op jit(solution)/shard_map/ppermute | solution.py:13
  43.7 21.3 %collective-permute-start.9 = (f32[16,12,4,128]{3,0,2,1:T(8,128)S(1)}, f32[16,12,4,128]{3,0,2,1:T(8,128)S(1)}, u32[]{:S(2)}, u32[]{:S(2)}) collective-permute-start(f32[16,12,4,128]{3,0,2,1:T(8,128)S(1)} %constant_dynamic-update-slice_fusion.3), channel_id=1, source_target_pairs={{2,0},{4,2},{6,4},{0,6},{3,1},{5,3},{7,5},{1,7},{10,8},{12,10},{14... | collective-permute-start | bytes 1179656 | tf_op jit(solution)/shard_map/ppermute | solution.py:16
  47.5 26.0 %collective-permute-start.2 = (f32[16,12,4,128]{3,0,2,1:T(8,128)S(1)}, f32[16,12,4,128]{3,0,2,1:T(8,128)}, u32[]{:S(2)}, u32[]{:S(2)}) collective-permute-start(f32[16,12,4,128]{3,0,2,1:T(8,128)S(1)} %constant_dynamic-update-slice_fusion), channel_id=1, source_target_pairs={{0,2},{2,4},{4,6},{6,0},{1,3},{3,5},{5,7},{7,1},{8,10},{10,12},{12... | collective-permute-start | bytes 1179656 | tf_op jit(solution)/shard_map/ppermute | solution.py:13
  47.6 31.5 %collective-permute-start.3 = (f32[16,12,4,128]{3,0,2,1:T(8,128)S(1)}, f32[16,12,4,128]{3,0,2,1:T(8,128)}, u32[]{:S(2)}, u32[]{:S(2)}) collective-permute-start(f32[16,12,4,128]{3,0,2,1:T(8,128)S(1)} %constant_dynamic-update-slice_fusion), channel_id=1, source_target_pairs={{2,0},{4,2},{6,4},{0,6},{3,1},{5,3},{7,5},{1,7},{10,8},{12,10},{14... | collective-permute-start | bytes 1179656 | tf_op jit(solution)/shard_map/ppermute | solution.py:16
  64.9 0.7 copy-start.1
  67.8 18.2 %collective-permute-start.10 = (f32[16,12,12,4]{0,3,2,1:T(4,128)}, f32[16,12,12,4]{0,3,2,1:T(4,128)}, u32[]{:S(2)}, u32[]{:S(2)}) collective-permute-start(f32[16,12,12,4]{0,3,2,1:T(4,128)} %copy.33), channel_id=1, source_target_pairs={{0,1},{1,0},{2,3},{3,2},{4,5},{5,4},{6,7},{7,6},{8,9},{9,8},{10,11... | collective-permute-start | bytes 110600 | tf_op jit(solution)/shard_map/ppermute | solution.py:13
  70.8 17.0 %collective-permute-start.11 = (f32[16,12,12,4]{0,3,2,1:T(4,128)}, f32[16,12,12,4]{0,3,2,1:T(4,128)}, u32[]{:S(2)}, u32[]{:S(2)}) collective-permute-start(f32[16,12,12,4]{0,3,2,1:T(4,128)} %copy.34), channel_id=1, source_target_pairs={{1,0},{0,1},{3,2},{2,3},{5,4},{4,5},{7,6},{6,7},{9,8},{8,9},{11,10... | collective-permute-start | bytes 110600 | tf_op jit(solution)/shard_map/ppermute | solution.py:16
  82.3 10.8 %collective-permute-start.4 = (f32[16,12,12,4]{0,3,2,1:T(4,128)}, f32[16,12,12,4]{0,3,2,1:T(4,128)}, u32[]{:S(2)}, u32[]{:S(2)}) collective-permute-start(f32[16,12,12,4]{0,3,2,1:T(4,128)} %copy.31), channel_id=1, source_target_pairs={{0,1},{1,0},{2,3},{3,2},{4,5},{5,4},{6,7},{7,6},{8,9},{9,8},{10,11... | collective-permute-start | bytes 110600 | tf_op jit(solution)/shard_map/ppermute | solution.py:13
  85.4 11.4 %collective-permute-start.5 = (f32[16,12,12,4]{0,3,2,1:T(4,128)}, f32[16,12,12,4]{0,3,2,1:T(4,128)}, u32[]{:S(2)}, u32[]{:S(2)}) collective-permute-start(f32[16,12,12,4]{0,3,2,1:T(4,128)} %copy.32), channel_id=1, source_target_pairs={{1,0},{0,1},{3,2},{2,3},{5,4},{4,5},{7,6},{6,7},{9,8},{8,9},{11,10... | collective-permute-start | bytes 110600 | tf_op jit(solution)/shard_map/ppermute | solution.py:16
  254.3 3.2 copy-start
Sparse Core Ops, SparseCore 0:
  261.8 134.3 reduce-scatter.1
where the time goes:
time: 407 us; the launch traced here: 404 us
  waiting for transfers between devices  168 us (41%)
  other arithmetic  137 us (34%)
  local copies, waits for them, and re-layouts  53.4 us (13%)
  starting transfers between devices  22.7 us (6%)
  between operations  14.3 us (4%)
  matrix products  7.54 us (2%)
    reduce_scatter x1, waiting for transfers between devices, on_device(): lax.psum_scatter(lax.dot_general(occ_rows * vir_rows, flat_potential, (((...  135 us
    add x32, other arithmetic, pair_block(): scalar * field_wide[4 + dimension] + field_wide[3] * slopes[dimension]  62.8 us
    dynamic_update_slice x16, other arithmetic, on_device(): lax.scan(pair_block, jnp.zeros((), jnp.float32), occ_wide)  26.2 us
    dynamic_slice x32, local copies, waits for them, and re-layouts, on_device(): lax.scan(pair_block, jnp.zeros((), jnp.float32), occ_wide)  22.4 us
    ppermute x9, waiting for transfers between devices, padded(): lax.ppermute(lax.slice_in_dim(block, 0, width, axis=dim), axis, backward)  20.4 us
    mul x16, other arithmetic, pair_block(): field_wide[5] * slopes[1]  16.4 us
    mul x16, other arithmetic, pair_block(): field_wide[4] * slopes[0] + field_wide[5] * slopes[1]  14.8 us
    ppermute x9, waiting for transfers between devices, padded(): lax.ppermute(lax.slice_in_dim(block, block.shape[dim] - width, None, axis...  13.5 us
  transfers between devices with their start and end apart: 19, of which 9 were waited for; matrix products, arithmetic and copies ran while one was open for 8% of the time, Pallas kernels for 0%

commit v1 on v0

v1 whole, which is shorter than its diff:
```python
import functools

import jax
import jax.numpy as jnp
from jax import lax
from jax.experimental import pallas as pl
from jax.experimental.pallas import tpu as pltpu
from jax.sharding import PartitionSpec as P

MESH = pl.DeviceIdType.MESH
F32 = jnp.float32
BF16 = jnp.bfloat16


def halo_kernel(orb, fld, zed, zfl, arms, corners, fx, fy, zz, zg, zx, zy, send, recv):
    nx, ny, nz = (lax.axis_size(a) for a in ("gx", "gy", "gz"))
    x, y, z = (lax.axis_index(a) for a in ("gx", "gy", "gz"))
    bx, by = orb.shape[0], orb.shape[1]
    up = lambda v, n: lax.rem(v + 1, n)
    dn = lambda v, n: lax.rem(v + n - 1, n)
    xs = (dn(x, nx), up(x, nx))
    ys = (dn(y, ny), up(y, ny))
    zs = (dn(z, nz), up(z, nz))

    def dev(gx=None, gy=None, gz=None):
        return {
            "gx": x if gx is None else gx,
            "gy": y if gy is None else gy,
            "gz": z if gz is None else gz,
        }

    barrier = pltpu.get_barrier_semaphore()
    others = [dev(gx=v) for v in xs] + [dev(gy=v) for v in ys] + [dev(gz=v) for v in zs]
    others += [dev(gx=v, gy=w) for v in xs for w in ys]
    for d in others:
        pl.semaphore_signal(barrier, inc=1, device_id=d, device_id_type=MESH)
    pl.semaphore_wait(barrier, len(others))

    copies = []

    def put(src, dst, device):
        k = len(copies)
        c = pltpu.make_async_remote_copy(
            src_ref=src,
            dst_ref=dst,
            send_sem=send.at[k],
            recv_sem=recv.at[k],
            device_id=device,
            device_id_type=MESH,
        )
        c.start()
        copies.append(c)

    for side in range(2):
        put(zed, zz.at[side], dev(gz=zs[1 - side]))
        put(zfl, zg.at[side], dev(gz=zs[1 - side]))
    first_z = list(copies)
    for side in range(2):
        lo_x = pl.ds(bx - 2, 2) if side == 0 else pl.ds(0, 2)
        lo_y = pl.ds(by - 2, 2) if side == 0 else pl.ds(0, 2)
        put(orb, arms.at[side], dev(gx=xs[1 - side]))
        put(orb, arms.at[2 + side], dev(gy=ys[1 - side]))
        put(fld.at[lo_x], fx.at[side], dev(gx=xs[1 - side]))
        put(fld.at[:, lo_y], fy.at[side], dev(gy=ys[1 - side]))
    for sx in range(2):
        for sy in range(2):
            lo_x = pl.ds(bx - 2, 2) if sx == 0 else pl.ds(0, 2)
            lo_y = pl.ds(by - 2, 2) if sy == 0 else pl.ds(0, 2)
            put(
                orb.at[lo_x, lo_y],
                corners.at[2 * sx + sy],
                dev(gx=xs[1 - sx], gy=ys[1 - sy]),
            )
    for c in first_z:
        c.wait()
    for side in range(2):
        lo_x = pl.ds(bx - 2, 2) if side == 0 else pl.ds(0, 2)
        lo_y = pl.ds(by - 2, 2) if side == 0 else pl.ds(0, 2)
        for zside in range(2):
            put(zz.at[zside, lo_x], zx.at[side, zside], dev(gx=xs[1 - side]))
            put(zz.at[zside, :, lo_y], zy.at[side, zside], dev(gy=ys[1 - side]))
    for c in copies[len(first_z):]:
        c.wait()


def main_kernel(
    norb, orb, fld, k0, arms, corners, fx, fy, zz, zg, zx, zy,
    pot, part,
    nS, oS, vS, vE, eF, C, A0, A1, f0, f1, f2, base, ph, plo, nh, nl,
):
    nocc, nvir = norb
    bx, by = orb.shape[0], orb.shape[1]
    lanes = orb.shape[3]
    i = pl.program_id(0)
    shifts = (1, -1, 2, -2)

    def src(x, y):
        inx, iny = 0 <= x < bx, 0 <= y < by
        if inx and iny:
            return orb.at[x, y]
        if iny:
            return arms.at[0, x + bx, y] if x < 0 else arms.at[1, x - bx, y]
        if inx:
            return arms.at[2, x, y + by] if y < 0 else arms.at[3, x, y - by]
        sx, sy = int(x >= 0), int(y >= 0)
        return corners.at[2 * sx + sy, x - bx if sx else x + 2, y - by if sy else y + 2]

    def zsrc(x, y, zside):
        inx, iny = 0 <= x < bx, 0 <= y < by
        if inx and iny:
            return zz.at[zside, x, y]
        if iny:
            return zx.at[0, zside, x + 2, y] if x < 0 else zx.at[1, zside, x - bx, y]
        return zy.at[0, zside, x, y + 2] if y < 0 else zy.at[1, zside, x, y - by]

    def fsrc(x, y):
        inx, iny = 0 <= x < bx, 0 <= y < by
        if inx and iny:
            return fld.at[x, y]
        if iny:
            return fx.at[0, x + 2, y] if x < 0 else fx.at[1, x - bx, y]
        return fy.at[0, x, y + 2] if y < 0 else fy.at[1, x, y - by]

    center = [(x, y) for x in range(bx) for y in range(by)]
    xarm = [(x, y) for x in (-2, -1, bx, bx + 1) for y in range(by)]
    yarm = [(x, y) for x in range(bx) for y in (-2, -1, by, by + 1)]
    near = center + xarm + yarm
    far = [(x, y) for x in (-4, -3, bx + 2, bx + 3) for y in range(by)]
    far += [(x, y) for x in range(bx) for y in (-4, -3, by + 2, by + 3)]
    far += [(x, y) for x in (-2, -1, bx, bx + 1) for y in (-2, -1, by, by + 1)]
    lane = lax.broadcasted_iota(jnp.int32, (nvir, lanes), 1)

    def slope(f):
        return 8.0 * (f(1) - f(-1)) - (f(2) - f(-2))

    @pl.when(i == 0)
    def _():
        lane1 = lax.broadcasted_iota(jnp.int32, (1, lanes), 1)
        upper = (lane1 & 7) < 4
        edge = (lane < 2) | (lane >= lanes - 2)

        row = lax.broadcasted_iota(jnp.int32, (nocc, lanes), 0)
        owner = lax.rem(((lane + 2) // 8) + row, lanes // 8) == 0

        def wrapped(s):
            return lane < s if s > 0 else lane >= lanes + s

        def spread(v):
            v = jnp.where(edge, v, 0.0)
            step = 8
            while step < lanes:
                v = v + pltpu.roll(v, step, 1)
                step *= 2
            return v

        for x, y in near:
            rows = jnp.where(upper, zsrc(x, y, 1)[...], zsrc(x, y, 0)[...])
            o_alt = pltpu.roll(
                jnp.broadcast_to(rows[0:1], (nocc, lanes)), 0, 1, stride=8, stride_axis=0
            )
            v_alt = pltpu.roll(
                jnp.broadcast_to(rows[1:2], (nvir, lanes)), 0, 1, stride=8, stride_axis=0
            )
            o_own = src(x, y)[0:nocc]
            v_own = src(x, y)[nocc:nocc + nvir]
            eS_v = spread(v_alt)
            vE[0, x + 2, y + 2] = rows[0:1] * eS_v
            middle = 0 <= x < bx and 0 <= y < by
            for k, s in enumerate(shifts):
                m = wrapped(s)
                roll = (-s) % lanes
                scale = 8.0 if abs(s) == 1 else 1.0
                oS[k, x + 2, y + 2] = scale * pltpu.roll(jnp.where(m, o_alt, o_own), roll, 1)
                vS[k, x + 2, y + 2] = pltpu.roll(jnp.where(m, v_alt, v_own), roll, 1)
                if middle:
                    oe = scale * pltpu.roll(jnp.where(m, o_own, o_alt), roll, 1)
                    ve = pltpu.roll(jnp.where(m, v_own, v_alt), roll, 1)
                    oe = jnp.where(owner, spread(oe), 0.0)
                    oe = jnp.sum(oe, axis=0, keepdims=True)
                    vE[1 + k, x + 2, y + 2] = oe * spread(ve)

        for x, y in center:
            g = jnp.where(upper, zg[1, x, y], zg[0, x, y])
            g0, g1, g2 = g[0:1], g[1:2], g[2:3]
            k1, k2, k3 = g[3:4], g[4:5], g[5:6]
            at = lambda dx, dy: vE[0, x + 2 + dx, y + 2 + dy]
            s0 = slope(lambda t: at(t, 0))
            s1 = slope(lambda t: at(0, t))
            s2 = (vE[1, x + 2, y + 2] - vE[2, x + 2, y + 2]) - (
                vE[3, x + 2, y + 2] - vE[4, x + 2, y + 2]
            )
            eF[x, y] = (
                (k2 * g2 * g0) * s0
                + (k2 * g2 * g1) * s1
                + (k2 * g2 * g2 + k3) * s2
                + (k1 * g2) * at(0, 0)
            )
        for x, y in center:
            f = fsrc(x, y)[...]
            for k in range(6):
                C[k, x, y] = jnp.broadcast_to(f[k:k + 1], (8, lanes))
            C[6, x, y] = jnp.broadcast_to(k0[x, y], (8, lanes))
        for arm, cells, me in ((A0, xarm, 0), (A1, yarm, 1)):
            for at, (x, y) in enumerate(cells):
                f = fsrc(x, y)[...]
                gm = f[me:me + 1]
                for k in range(3):
                    c = f[4:5] * gm * f[k:k + 1]
                    if k == me:
                        c = c + f[5:6]
                    arm[k, at] = jnp.broadcast_to(c, (8, lanes))
                arm[3, at] = jnp.broadcast_to(f[3:4] * gm, (8, lanes))

    def rows2(c):
        return jnp.concatenate([c] * (nvir // 8), axis=0)

    off = 4
    for x, y in near + far:
        cell = src(x, y)
        nS[x + off, y + off] = cell[pl.ds(i, 1)] * cell[nocc:nocc + nvir]

    def n_at(x, y):
        return nS[x + off, y + off]

    def slopes(x, y):
        s0 = slope(lambda t: n_at(x + t, y))
        s1 = slope(lambda t: n_at(x, y + t))
        p = [oS[k, x + 2, y + 2, pl.ds(i, 1)] * vS[k, x + 2, y + 2] for k in range(4)]
        return s0, s1, (p[0] - p[1]) - (p[2] - p[3])

    for arm, cells, out in ((A0, xarm, f0), (A1, yarm, f1)):
        for at, (x, y) in enumerate(cells):
            s0, s1, s2 = slopes(x, y)
            value = (
                rows2(arm[0, at]) * s0
                + rows2(arm[1, at]) * s1
                + rows2(arm[2, at]) * s2
                + rows2(arm[3, at]) * n_at(x, y)
            )
            if out is f0:
                f0[x + 2, y] = value
            else:
                f1[x, y + 2] = value

    back = 8 * i
    row0 = pl.multiple_of(i * nvir, nvir)
    for x, y in center:
        s0, s1, s2 = slopes(x, y)
        g0, g1, g2, k1, k2, k3, kk = (rows2(C[k, x, y]) for k in range(7))
        n = n_at(x, y)
        al = g0 * s0 + g1 * s1 + g2 * s2
        sc = k1 * n + k2 * al
        f0[x + 2, y] = sc * g0 + k3 * s0
        f1[x, y + 2] = sc * g1 + k3 * s1
        f = sc * g2 + k3 * s2
        e = pltpu.roll(eF[x, y], back, 1)
        up1 = pltpu.roll(jnp.where(lane < 1, e, f), lanes - 1, 1)
        up2 = pltpu.roll(jnp.where(lane < 2, e, f), lanes - 2, 1)
        dn1 = pltpu.roll(jnp.where(lane >= lanes - 1, e, f), 1, 1)
        dn2 = pltpu.roll(jnp.where(lane >= lanes - 2, e, f), 2, 1)
        base[x, y] = kk * n + k1 * al - (8.0 * (up1 - dn1) - (up2 - dn2))
        at = (x * by + y) * lanes
        hi = n.astype(BF16)
        nh[pl.ds(row0, nvir), at:at + lanes] = hi
        nl[pl.ds(row0, nvir), at:at + lanes] = (n - hi.astype(F32)).astype(BF16)

    for x, y in center:
        inner = (f0[x + 3, y] - f0[x + 1, y]) + (f1[x, y + 3] - f1[x, y + 1])
        outer = (f0[x + 4, y] - f0[x, y]) + (f1[x, y + 4] - f1[x, y])
        v = base[x, y] - (8.0 * inner - outer)
        cell = x * by + y
        pot[pl.ds(cell, nvir, stride=bx * by), :] = v
        at = cell * lanes
        hi = v.astype(BF16)
        ph[pl.ds(row0, nvir), at:at + lanes] = hi
        plo[pl.ds(row0, nvir), at:at + lanes] = (v - hi.astype(F32)).astype(BF16)

    @pl.when(i == nocc - 1)
    def _():
        def dot(a, b):
            return lax.dot_general(
                a[...], b[...], (((1,), (1,)), ((), ())), preferred_element_type=F32
            )

        part[...] = dot(nh, ph) + dot(nh, plo) + dot(nl, ph)


def scatter_kernel(scale, part, out, got, send, recv):
    nx, ny, nz = (lax.axis_size(a) for a in ("gx", "gy", "gz"))
    n = nx * ny * nz
    me = (lax.axis_index("gx") * ny + lax.axis_index("gy")) * nz + lax.axis_index("gz")

    def dev(d):
        t = lax.rem(me + d, n)
        return t, {"gx": t // (ny * nz), "gy": lax.rem(t // nz, ny), "gz": lax.rem(t, nz)}

    barrier = pltpu.get_barrier_semaphore()

    def greet(d, c):
        pl.semaphore_signal(barrier, inc=1, device_id=dev(d)[1], device_id_type=MESH)
        return c

    lax.fori_loop(1, n, greet, 0)
    pl.semaphore_wait(barrier, n - 1)

    def copy(d):
        t, target = dev(d)
        return pltpu.make_async_remote_copy(
            src_ref=part.at[t],
            dst_ref=got.at[d],
            send_sem=send.at[d],
            recv_sem=recv.at[d],
            device_id=target,
            device_id_type=MESH,
        )

    def start(d, c):
        copy(d).start()
        return c

    lax.fori_loop(1, n, start, 0)
    out[...] = part[me]

    def take(d, c):
        copy(d).wait()
        out[...] += got[d]
        return c

    lax.fori_loop(1, n, take, 0)
    out[...] = out[...] * scale


def on_device(occupied, virtual, kernel_fields, density_grad):
    nocc, bx, by, lanes = occupied.shape
    nvir = virtual.shape[0]
    devices = lax.axis_size("gx") * lax.axis_size("gy") * lax.axis_size("gz")
    by_cell = lambda a: jnp.transpose(a, (1, 2, 0, 3))
    orb = by_cell(jnp.concatenate([occupied, virtual], axis=0))
    coefs = jnp.concatenate(
        [
            density_grad,
            kernel_fields[1:2] / 12.0,
            kernel_fields[2:4] / 144.0,
            jnp.zeros_like(density_grad[0:2]),
        ],
        axis=0,
    )
    fld = by_cell(coefs)
    k0 = kernel_fields[0][:, :, None, :]

    def slots(a):
        turned = a[::-1]
        lo = jnp.roll(turned[..., :4], 1, axis=0)
        hi = turned[..., lanes - 4:]
        return jnp.transpose(jnp.concatenate([lo, hi], axis=-1), (1, 2, 0, 3)).reshape(bx, by, -1)

    zed = jnp.stack([slots(occupied), slots(virtual)], axis=2)
    ends = jnp.concatenate([fld[..., :4], fld[..., lanes - 4:]], axis=-1)
    zfl = jnp.tile(ends, (1, 1, 1, lanes // 8))

    sds = lambda *s: jax.ShapeDtypeStruct(s, F32)
    norb = nocc + nvir
    halo_shapes = (
        sds(4, bx, by, norb, lanes),
        sds(4, 2, 2, norb, lanes),
        sds(2, 2, by, 8, lanes),
        sds(2, bx, 2, 8, lanes),
        sds(2, bx, by, 2, lanes),
        sds(2, bx, by, 8, lanes),
        sds(2, 2, 2, by, 2, lanes),
        sds(2, 2, bx, 2, 2, lanes),
    )
    vmem = pl.BlockSpec(memory_space=pltpu.VMEM)
    halos = pl.pallas_call(
        halo_kernel,
        out_shape=halo_shapes,
        in_specs=[vmem] * 4,
        out_specs=[vmem] * 8,
        scratch_shapes=[pltpu.SemaphoreType.DMA((24,)), pltpu.SemaphoreType.DMA((24,))],
        compiler_params=pltpu.CompilerParams(collective_id=0, has_side_effects=True),
        name="halo",
    )(orb, fld, zed, zfl)

    cells = bx * by * lanes
    pairs = nocc * nvir
    wide = lambda *s: pltpu.VMEM(s + (nvir, lanes), F32)
    pot, part = pl.pallas_call(
        functools.partial(main_kernel, (nocc, nvir)),
        grid=(nocc,),
        out_shape=(sds(pairs * bx * by, lanes), sds(pairs, pairs)),
        in_specs=[vmem] * 11,
        out_specs=(
            pl.BlockSpec((nvir * bx * by, lanes), lambda i: (i, 0)),
            pl.BlockSpec((pairs, pairs), lambda i: (0, 0)),
        ),
        scratch_shapes=[
            wide(bx + 8, by + 8),
            pltpu.VMEM((4, bx + 4, by + 4, nocc, lanes), F32),
            wide(4, bx + 4, by + 4),
            wide(5, bx + 4, by + 4),
            wide(bx, by),
            pltpu.VMEM((7, bx, by, 8, lanes), F32),
            pltpu.VMEM((4, 4 * by, 8, lanes), F32),
            pltpu.VMEM((4, 4 * bx, 8, lanes), F32),
            wide(bx + 4, by),
            wide(bx, by + 4),
            wide(1),
            wide(bx, by),
        ]
        + [pltpu.VMEM((pairs, cells), BF16)] * 4,
        compiler_params=pltpu.CompilerParams(
            dimension_semantics=("arbitrary",), vmem_limit_bytes=50 * 1024 * 1024
        ),
        name="response",
    )(orb, fld, k0, *halos)

    rows = pairs // devices
    casida = pl.pallas_call(
        functools.partial(scatter_kernel, 1.0 / (cells * devices)),
        out_shape=sds(rows, pairs),
        in_specs=[vmem],
        out_specs=vmem,
        scratch_shapes=[
            pltpu.VMEM((devices, rows, pairs), F32),
            pltpu.SemaphoreType.DMA((devices,)),
            pltpu.SemaphoreType.DMA((devices,)),
        ],
        compiler_params=pltpu.CompilerParams(collective_id=1, has_side_effects=True),
        name="scatter",
    )(part.reshape(devices, rows, pairs))
    return pot.reshape(pairs, bx, by, lanes), casida


def solution(mesh):
    spec = P(None, "gx", "gy", "gz")
    return jax.shard_map(
        on_device,
        mesh=mesh,
        in_specs=(spec,) * 4,
        out_specs=(spec, P(("gx", "gy", "gz"), None)),
        check_vma=False,
    )
```

time: 407 us -> 119 us (0.29)
  waiting for transfers between devices: 168 us -> 0 us
  other arithmetic: 137 us -> 2.44 us
  Pallas kernels: 0 us -> 95.2 us
  local copies, waits for them, and re-layouts: 53.4 us -> 19.2 us
  starting transfers between devices: 22.7 us -> 0 us
  between operations: 14.3 us -> 0.82 us
  matrix products: 7.54 us -> 0 us
    reduce_scatter x1 -> x0, waiting for transfers between devices: 135 us -> none  [on_device(): lax.psum_scatter(lax.dot_general(occ_rows * vir_rows, flat_potential, (((...]
    pallas_call x0 -> x3, Pallas kernels: none -> 95.2 us  [the longest x1 52.6 us: on_device(): pl.pallas_call(functools.partial(main_kernel, (nocc, nvir)), grid=(nocc,)...]
    add x32 -> x0, other arithmetic: 62.8 us -> none  [pair_block(): scalar * field_wide[4 + dimension] + field_wide[3] * slopes[dimension]]
    mul x49 -> x0, other arithmetic: 39.4 us -> none  [the longest x16 16.4 us: pair_block(): field_wide[5] * slopes[1]]
    ppermute x18 -> x0, waiting for transfers between devices: 33.9 us -> none  [the longest x9 20.4 us: padded(): lax.ppermute(lax.slice_in_dim(block, 0, width, axis=dim), axis, backward)]
    dynamic_update_slice x16 -> x0, other arithmetic: 26.2 us -> none  [on_device(): lax.scan(pair_block, jnp.zeros((), jnp.float32), occ_wide)]
    ppermute x18 -> x0, starting transfers between devices: 22.6 us -> none  [the longest x9 13.5 us: padded(): lax.ppermute(lax.slice_in_dim(block, 0, width, axis=dim), axis, backward)]
    dynamic_slice x32 -> x0, local copies, waits for them, and re-layouts: 22.4 us -> none  [on_device(): lax.scan(pair_block, jnp.zeros((), jnp.float32), occ_wide)]
  transfers between devices with their start and end apart: 19 -> 0, of which waited for: 9 -> 0; matrix products, arithmetic and copies ran while one was open for 8% -> 0% of each run, Pallas kernels for 0% -> 0%
where the time goes in v1:
time: 119 us; the launch traced here: 118 us
  Pallas kernels  95.2 us (80%)
  local copies, waits for them, and re-layouts  19.2 us (16%)
  other arithmetic  2.44 us (2%)
    pallas_call x1, Pallas kernels, on_device(): pl.pallas_call(functools.partial(main_kernel, (nocc, nvir)), grid=(nocc,)...  52.6 us
    pallas_call x1, Pallas kernels, on_device(): pl.pallas_call(halo_kernel, out_shape=halo_shapes, in_specs=[vmem] * 4, o...  29.1 us
    pallas_call x1, Pallas kernels, on_device(): pl.pallas_call(functools.partial(scatter_kernel, 1.0 / (cells * devices))...  13.4 us
    unnamed x36, local copies, waits for them, and re-layouts  12 us
    slice x6, local copies, waits for them, and re-layouts, slots(): lo = jnp.roll(turned[..., :4], 1, axis=0)  3.46 us

profile of v1, /device:TPU:0, one launch (start us, length us, event | category | flops | bytes accessed | tf_op | source)
XLA Modules:
  0.0 117.7 jit_solution(6468654945911904716)
XLA Ops:
  0.6 0.0 copy-start.12
  0.7 0.1 pad.13.clone
  0.7 0.7 slice.60
  1.4 0.7 slice.65
  2.1 0.7 slice.58
  2.9 0.7 fusion.1
  3.6 0.2 copy.59
  3.8 0.2 copy.56
  4.0 0.8 copy.43
  4.7 0.1 maximum_bitcast_fusion.1.fld
  4.8 0.0 copy-start.1
  4.8 0.9 slice.61
  5.8 0.2 copy.57
  6.0 0.1 slice.62
  6.1 0.9 slice.66
  7.0 0.2 copy.60
  7.2 0.1 slice.67
  7.3 1.0 copy.40
  8.3 1.0 slice.63
  9.3 0.2 copy.58
  9.5 0.1 slice.64
  9.6 0.1 maximum_bitcast_fusion.2
  9.7 0.1 copy.48
  9.8 0.1 stack_reshape.6
  9.9 0.0 copy-done.12
  10.0 0.7 maximum_bitcast_fusion.orb
  10.7 0.0 copy-start
  10.7 0.1 slice.68
  10.8 0.2 copy.61
  11.0 0.1 slice.69
  11.1 0.1 maximum_bitcast_fusion.3
  11.2 0.1 copy.52
  11.3 0.1 stack_reshape.7
  11.5 0.6 pad_maximum_fusion.1.zed
  12.1 0.1 fusion
  12.2 0.0 copy-done.1
  12.2 0.0 copy-start.2
  12.2 0.1 pad_maximum_fusion
  12.3 0.1 tile.4
  12.4 1.1 tile.10.zfl
  13.4 29.1 %halo.1 = (f32[4,4,4,32,128]{4,3,2,1,0:T(8,128)}, f32[4,2,2,32,128]{4,3,2,1,0:T(8,128)}, f32[2,2,4,8,128]{4,3,2,1,0:T(8,128)}, f32[2,4,2,8,128]{4,3,2,1,0:T(8,12...) custom-call(f32[4,4,32,128]{3,2,1,0:T(8,128)} %maximum_bitcast_fusio, ...), custom_call_target="tpu_custom_call" | custom-call | tf_op jit(solution)/shard_map/halo/pallas_call | solution.py:374
  42.5 0.0 copy-done
  42.6 0.0 copy-done.2
  42.6 0.0 copy-start.3
  42.6 1.2 %copy-done.3 = f32[4,4,4,32,128]{4,3,2,1,0:T(8,128)S(1)} copy-done((f32[4,4,4,32,128]{4,3,2,1,0:T(8,128)S(1)}, f32[4,4,4,32,128]{4,3,2,1,0:T(8,128)}, u32[]{:S(2)}) %copy-start.3) | copy-done | bytes 1048600
  43.8 0.0 copy-start.4
  43.8 0.9 copy-done.4
  44.7 0.0 copy-start.6
  44.7 0.9 copy-done.6
  45.7 0.0 copy-start.7
  45.7 0.8 copy-done.7
  46.5 0.0 copy-start.8
  46.5 0.8 copy-done.8
  47.3 0.0 copy-start.9
  47.3 0.8 copy-done.9
  48.1 0.0 copy-start.10
  48.1 0.8 copy-done.10
  48.8 0.0 copy-start.11
  48.8 0.8 copy-done.11
  49.6 52.6 %response.1 = (f32[4096,128]{1,0:T(8,128)}, f32[256,256]{1,0:T(8,128)S(1)}) custom-call(f32[4,4,32,128]{3,2,1,0:T(8,128)S(1)} %copy-done, f32[4,4,8,128]{3,2,1,0:T(8,128)S(1)} %copy-done.2, f32[4,4,1,128]{3,2,1,0:T(1,128)S(1)} %bitcast.21, f32[4,4,4,32,128]{4,3,2,1,0:T(8,128)S(1)} %copy-done.3, f32[4,2,2,32,128]{4,3,2,1,0:T(8,128)S(1)} %copy-done.4, ...), custom_call_target="tpu_custom_call" | custom-call | tf_op jit(solution)/shard_map/response/pallas_call | solution.py:387
  102.2 0.0 copy-start.5
  102.2 0.7 copy-done.5
  102.9 13.4 %scatter.1 = f32[8,256]{1,0:T(8,128)} custom-call(f32[32,8,256]{2,1,0:T(8,128)} %bitcast.20), custom_call_target="tpu_custom_call" | custom-call | tf_op jit(solution)/shard_map/scatter/pallas_call | solution.py:418
  116.4 1.3 %copy.64 = f32[8,256]{1,0:T(8,128)} copy(f32[8,256]{1,0:T(8,128)} %scatter.1) | data formatting | bytes 16384
  (3 shorter events, 0.1 us)
Async XLA Ops:
  0.6 9.3 %copy-start.12 = (f32[16,4,4,128]{3,2,1,0:T(4,128)S(1)}, f32[16,4,4,128]{3,2,1,0:T(4,128)}, u32[]{:S(2)}) copy-start(f32[16,4,4,128]{3,2,1,0:T(4,128)} %param.5) | copy-start | bytes 393220
  4.8 7.3 %copy-start.1 = (f32[4,4,8,128]{3,2,1,0:T(8,128)}, f32[4,4,8,128]{3,2,1,0:T(8,128)S(1)}, u32[]{:S(2)}) copy-start(f32[4,4,8,128]{3,2,1,0:T(8,128)S(1)} %maximum_bitcast_fusion.1.fld) | copy-start | bytes 196612
  10.7 31.8 %copy-start = (f32[4,4,32,128]{3,2,1,0:T(8,128)S(1)}, f32[4,4,32,128]{3,2,1,0:T(8,128)}, u32[]{:S(2)}) copy-start(f32[4,4,32,128]{3,2,1,0:T(8,128)} %maximum_bitcast_fusion.orb) | copy-start | bytes 786436
  12.2 30.4 %copy-start.2 = (f32[4,4,8,128]{3,2,1,0:T(8,128)S(1)}, f32[4,4,8,128]{3,2,1,0:T(8,128)}, u32[]{:S(2)}) copy-start(f32[4,4,8,128]{3,2,1,0:T(8,128)} %copy-done.1) | copy-start | bytes 196612
  42.6 1.2 %copy-start.3 = (f32[4,4,4,32,128]{4,3,2,1,0:T(8,128)S(1)}, f32[4,4,4,32,128]{4,3,2,1,0:T(8,128)}, u32[]{:S(2)}) copy-start(f32[4,4,4,32,128]{4,3,2,1,0:T(8,128)} %get-tuple-element.12.arms) | copy-start | bytes 3145732
  43.8 0.9 copy-start.4
  44.7 0.9 copy-start.6
  45.7 0.8 copy-start.7
  46.5 0.8 copy-start.8
  47.3 0.8 copy-start.9
  48.1 0.8 copy-start.10
  48.8 0.8 copy-start.11
  102.2 0.7 copy-start.5

commit v2 on v1

v2 whole, which is shorter than its diff:
```python
import functools

import jax
import jax.numpy as jnp
from jax import lax
from jax.experimental import pallas as pl
from jax.experimental.pallas import tpu as pltpu
from jax.sharding import PartitionSpec as P

MESH = pl.DeviceIdType.MESH
F32 = jnp.float32
BF16 = jnp.bfloat16


def spread(v, lane):
    lanes = v.shape[1]
    v = jnp.where((lane < 4) | (lane >= lanes - 4), v, 0.0)
    step = 8
    while step < lanes:
        v = v + pltpu.roll(v, step, 1)
        step *= 2
    return v


def slot_owner(shape):
    lane = lax.broadcasted_iota(jnp.int32, shape, 1)
    row = lax.broadcasted_iota(jnp.int32, shape, 0)
    return lax.rem(((lane + 4) // 8) + row, shape[1] // 8) == 0


def prep_kernel(cells, occ, vir, ker, grd, orb, fld, zed, zfl):
    lanes = occ.shape[1]
    nocc, nvir = occ.shape[0] // cells, vir.shape[0] // cells

    def cell(c, carry):
        for k, (ref, count, at) in enumerate(((occ, nocc, 0), (vir, nvir, nocc))):
            rows = ref[pl.ds(c, count, stride=cells), :]
            orb[c, at:at + count] = rows
            lane = lax.broadcasted_iota(jnp.int32, rows.shape, 1)
            packed = jnp.where(slot_owner(rows.shape), spread(rows, lane), 0.0)
            zed[c, k:k + 1] = jnp.sum(packed, axis=0, keepdims=True)
        g = [grd[pl.ds(k * cells + c, 1), :] for k in range(3)]
        f = [ker[pl.ds(k * cells + c, 1), :] for k in range(4)]
        rows = g + [f[1] * (1.0 / 12.0), f[2] * (1.0 / 144.0), f[3] * (1.0 / 144.0), f[0], f[0]]
        eight = jnp.concatenate(rows, axis=0)
        fld[c] = eight
        zfl[c] = spread(eight, lax.broadcasted_iota(jnp.int32, eight.shape, 1))
        return carry

    lax.fori_loop(0, cells, cell, 0)


def halo_kernel(orb, fld, zed, zfl, wide, wfld, wz, wg, send, recv, own):
    nx, ny, nz = (lax.axis_size(a) for a in ("gx", "gy", "gz"))
    x, y, z = (lax.axis_index(a) for a in ("gx", "gy", "gz"))
    bx, by = orb.shape[0], orb.shape[1]
    up = lambda v, n: lax.rem(v + 1, n)
    dn = lambda v, n: lax.rem(v + n - 1, n)
    xs = (dn(x, nx), up(x, nx))
    ys = (dn(y, ny), up(y, ny))
    zs = (dn(z, nz), up(z, nz))

    def dev(gx=None, gy=None, gz=None):
        return {
            "gx": x if gx is None else gx,
            "gy": y if gy is None else gy,
            "gz": z if gz is None else gz,
        }

    barrier = pltpu.get_barrier_semaphore()
    others = [dev(gx=v) for v in xs] + [dev(gy=v) for v in ys] + [dev(gz=v) for v in zs]
    for d in others:
        pl.semaphore_signal(barrier, inc=1, device_id=d, device_id_type=MESH)
    pl.semaphore_wait(barrier, len(others))

    copies = []

    def put(src, dst, device):
        k = len(copies)
        c = pltpu.make_async_remote_copy(
            src_ref=src,
            dst_ref=dst,
            send_sem=send.at[k],
            recv_sem=recv.at[k],
            device_id=device,
            device_id_type=MESH,
        )
        c.start()
        copies.append(c)
        return c

    def edge(b, side, width):
        return pl.ds(b - width, width) if side == 0 else pl.ds(0, width)

    def rim(b, side, width, margin):
        return pl.ds(margin - width, width) if side == 0 else pl.ds(b + margin, width)

    in_x, in_y = pl.ds(4, bx), pl.ds(4, by)
    mid_x, mid_y = pl.ds(2, bx), pl.ds(2, by)
    near = [
        put(
            orb.at[:, edge(by, side, 2)],
            wide.at[in_x, rim(by, side, 2, 4)],
            dev(gy=ys[1 - side]),
        )
        for side in range(2)
    ]
    zc = []
    for side in range(2):
        zc.append(put(zed, wz.at[side, mid_x, mid_y], dev(gz=zs[1 - side])))
        put(zfl, wg.at[side], dev(gz=zs[1 - side]))
    for side in range(2):
        put(
            orb,
            wide.at[pl.ds(0, bx) if side == 0 else pl.ds(bx + 4, bx), in_y],
            dev(gx=xs[1 - side]),
        )
        far_src = pl.ds(by - 4, 2) if side == 0 else pl.ds(2, 2)
        far_dst = pl.ds(0, 2) if side == 0 else pl.ds(by + 6, 2)
        put(orb.at[:, far_src], wide.at[in_x, far_dst], dev(gy=ys[1 - side]))
        put(
            fld.at[edge(bx, side, 2)],
            wfld.at[rim(bx, side, 2, 2), mid_y],
            dev(gx=xs[1 - side]),
        )
        put(
            fld.at[:, edge(by, side, 2)],
            wfld.at[mid_x, rim(by, side, 2, 2)],
            dev(gy=ys[1 - side]),
        )
    mine = [
        pltpu.make_async_copy(orb, wide.at[in_x, in_y], own.at[0]),
        pltpu.make_async_copy(fld, wfld.at[mid_x, mid_y], own.at[1]),
    ]
    for c in mine:
        c.start()
    for c in zc:
        c.wait_recv()
    last = []
    for side in range(2):
        own_x = pl.ds(bx, 2) if side == 0 else pl.ds(2, 2)
        own_y = pl.ds(by, 2) if side == 0 else pl.ds(2, 2)
        for k in range(2):
            last.append(
                put(
                    wz.at[k, own_x, mid_y],
                    wz.at[k, rim(bx, side, 2, 2), mid_y],
                    dev(gx=xs[1 - side]),
                )
            )
            last.append(
                put(
                    wz.at[k, mid_x, own_y],
                    wz.at[k, mid_x, rim(by, side, 2, 2)],
                    dev(gy=ys[1 - side]),
                )
            )
    for sy in range(2):
        near[sy].wait_recv()
        for sx in range(2):
            own_x = pl.ds(bx + 2, 2) if sx == 0 else pl.ds(4, 2)
            rim_y = rim(by, sy, 2, 4)
            put(
                wide.at[own_x, rim_y],
                wide.at[rim(bx, sx, 2, 4), rim_y],
                dev(gx=xs[1 - sx]),
            )
    early = near + zc
    for c in early:
        c.wait_send()
    for c in copies:
        if not any(c is e for e in early):
            c.wait()
    for c in mine:
        c.wait()


def main_kernel(
    norb, wide, wfld, wz, wg,
    pot, part,
    nS, oS, vS, vE, eF, C, A0, A1, f0, f1, f2, base, ph, plo, nh, nl,
):
    nocc, nvir = norb
    bx, by = wide.shape[0] - 8, wide.shape[1] - 8
    lanes = wide.shape[3]
    i = pl.program_id(0)
    shifts = (1, -1, 2, -2)

    center = [(x, y) for x in range(bx) for y in range(by)]
    xarm = [(x, y) for x in (-2, -1, bx, bx + 1) for y in range(by)]
    yarm = [(x, y) for x in range(bx) for y in (-2, -1, by, by + 1)]
    near = center + xarm + yarm
    far = [(x, y) for x in (-4, -3, bx + 2, bx + 3) for y in range(by)]
    far += [(x, y) for x in range(bx) for y in (-4, -3, by + 2, by + 3)]
    far += [(x, y) for x in (-2, -1, bx, bx + 1) for y in (-2, -1, by, by + 1)]
    lane = lax.broadcasted_iota(jnp.int32, (nvir, lanes), 1)

    def slope(f):
        return 8.0 * (f(1) - f(-1)) - (f(2) - f(-2))

    @pl.when(i == 0)
    def _():
        lane1 = lax.broadcasted_iota(jnp.int32, (1, lanes), 1)
        upper = (lane1 & 7) < 4
        owner = slot_owner((nocc, lanes))

        def wrapped(s):
            return lane < s if s > 0 else lane >= lanes + s

        def pair(x, y):
            rows = jnp.where(upper, wz[1, x, y], wz[0, x, y])
            alt = [
                pltpu.roll(
                    jnp.broadcast_to(rows[k:k + 1], (n, lanes)), 0, 1, stride=8, stride_axis=0
                )
                for k, n in enumerate((nocc, nvir))
            ]
            return rows, alt, wide[x + 2, y + 2, 0:nocc], wide[x + 2, y + 2, nocc:nocc + nvir]

        def prepare(x, y):
            rows, (o_alt, v_alt), o_own, v_own = pair(x, y)
            vE[0, x, y] = rows[0:1] * spread(v_alt, lane)
            for k, s in enumerate(shifts):
                m = wrapped(s)
                roll = (-s) % lanes
                scale = 8.0 if abs(s) == 1 else 1.0
                oS[k, x, y] = scale * pltpu.roll(jnp.where(m, o_alt, o_own), roll, 1)
                vS[k, x, y] = pltpu.roll(jnp.where(m, v_alt, v_own), roll, 1)

        def band(t, c):
            prepare(t // by, 2 + lax.rem(t, by))
            return c

        lax.fori_loop(0, (bx + 4) * by, band, 0)

        def sides(t, c):
            y = lax.rem(t, 4)
            prepare(2 + t // 4, jnp.where(y < 2, y, y + by))
            return c

        lax.fori_loop(0, bx * 4, sides, 0)

        def flux_at(me, f, s, n):
            g = [f[k:k + 1] for k in range(3)]
            total = (f[3:4] * g[me]) * n
            for k in range(3):
                c = f[4:5] * g[me] * g[k]
                total += (c + f[5:6] if k == me else c) * s[k]
            return total

        def edges(t, carry):
            x, y = t // by + 2, lax.rem(t, by) + 2
            rows, (o_alt, v_alt), o_own, v_own = pair(x, y)
            p = []
            for k, s in enumerate(shifts):
                m = wrapped(s)
                roll = (-s) % lanes
                oe = spread(pltpu.roll(jnp.where(m, o_own, o_alt), roll, 1), lane)
                ve = spread(pltpu.roll(jnp.where(m, v_own, v_alt), roll, 1), lane)
                oe = jnp.sum(jnp.where(owner, oe, 0.0), axis=0, keepdims=True)
                p.append(oe * ve)
            s2 = 8.0 * (p[0] - p[1]) - (p[2] - p[3])
            s0 = slope(lambda d: vE[0, x + d, y])
            s1 = slope(lambda d: vE[0, x, y + d])
            g = jnp.where(upper, wg[1, x - 2, y - 2], wg[0, x - 2, y - 2])
            eF[x - 2, y - 2] = flux_at(2, g, (s0, s1, s2), vE[0, x, y])
            f = wfld[x, y]
            for k in range(7):
                C[k, x - 2, y - 2] = jnp.broadcast_to(f[k:k + 1], (8, lanes))
            return carry

        lax.fori_loop(0, bx * by, edges, 0)

        def arm_coefs(arm, at, me, f):
            gm = f[me:me + 1]
            for k in range(3):
                c = f[4:5] * gm * f[k:k + 1]
                if k == me:
                    c = c + f[5:6]
                arm[k, at] = jnp.broadcast_to(c, (8, lanes))
            arm[3, at] = jnp.broadcast_to(f[3:4] * gm, (8, lanes))

        def arm_x(t, c):
            x = t // by
            arm_coefs(A0, t, 0, wfld[jnp.where(x < 2, x, x + bx), 2 + lax.rem(t, by)])
            return c

        lax.fori_loop(0, 4 * by, arm_x, 0)

        def arm_y(t, c):
            y = lax.rem(t, 4)
            arm_coefs(A1, t, 1, wfld[2 + t // 4, jnp.where(y < 2, y, y + by)])
            return c

        lax.fori_loop(0, 4 * bx, arm_y, 0)

    def rows2(c):
        return jnp.concatenate([c] * (nvir // 8), axis=0)

    off = 4
    for x, y in near + far:
        cell = wide.at[x + off, y + off]
        nS[x + off, y + off] = cell[pl.ds(i, 1)] * cell[nocc:nocc + nvir]

    def n_at(x, y):
        return nS[x + off, y + off]

    def slopes(x, y):
        s0 = slope(lambda t: n_at(x + t, y))
        s1 = slope(lambda t: n_at(x, y + t))
        p = [oS[k, x + 2, y + 2, pl.ds(i, 1)] * vS[k, x + 2, y + 2] for k in range(4)]
        return s0, s1, (p[0] - p[1]) - (p[2] - p[3])

    for arm, cells, out in ((A0, xarm, f0), (A1, yarm, f1)):
        for at, (x, y) in enumerate(cells):
            s0, s1, s2 = slopes(x, y)
            value = (
                rows2(arm[0, at]) * s0
                + rows2(arm[1, at]) * s1
                + rows2(arm[2, at]) * s2
                + rows2(arm[3, at]) * n_at(x, y)
            )
            if out is f0:
                f0[x + 2, y] = value
            else:
                f1[x, y + 2] = value

    back = 8 * i
    row0 = pl.multiple_of(i * nvir, nvir)
    for x, y in center:
        s0, s1, s2 = slopes(x, y)
        g0, g1, g2, k1, k2, k3, kk = (rows2(C[k, x, y]) for k in range(7))
        n = n_at(x, y)
        al = g0 * s0 + g1 * s1 + g2 * s2
        sc = k1 * n + k2 * al
        f0[x + 2, y] = sc * g0 + k3 * s0
        f1[x, y + 2] = sc * g1 + k3 * s1
        f = sc * g2 + k3 * s2
        e = pltpu.roll(eF[x, y], back, 1)
        up1 = pltpu.roll(jnp.where(lane < 1, e, f), lanes - 1, 1)
        up2 = pltpu.roll(jnp.where(lane < 2, e, f), lanes - 2, 1)
        dn1 = pltpu.roll(jnp.where(lane >= lanes - 1, e, f), 1, 1)
        dn2 = pltpu.roll(jnp.where(lane >= lanes - 2, e, f), 2, 1)
        base[x, y] = kk * n + k1 * al - (8.0 * (up1 - dn1) - (up2 - dn2))
        at = (x * by + y) * lanes
        hi = n.astype(BF16)
        nh[pl.ds(row0, nvir), at:at + lanes] = hi
        nl[pl.ds(row0, nvir), at:at + lanes] = (n - hi.astype(F32)).astype(BF16)

    for x, y in center:
        inner = (f0[x + 3, y] - f0[x + 1, y]) + (f1[x, y + 3] - f1[x, y + 1])
        outer = (f0[x + 4, y] - f0[x, y]) + (f1[x, y + 4] - f1[x, y])
        v = base[x, y] - (8.0 * inner - outer)
        cell = x * by + y
        pot[pl.ds(cell, nvir, stride=bx * by), :] = v
        at = cell * lanes
        hi = v.astype(BF16)
        ph[pl.ds(row0, nvir), at:at + lanes] = hi
        plo[pl.ds(row0, nvir), at:at + lanes] = (v - hi.astype(F32)).astype(BF16)

    @pl.when(i == nocc - 1)
    def _():
        def dot(a, b):
            return lax.dot_general(
                a[...], b[...], (((1,), (1,)), ((), ())), preferred_element_type=F32
            )

        part[...] = dot(nh, ph) + dot(nh, plo) + dot(nl, ph)


def scatter_kernel(scale, part, out, got, send, recv):
    nx, ny, nz = (lax.axis_size(a) for a in ("gx", "gy", "gz"))
    n = nx * ny * nz
    me = (lax.axis_index("gx") * ny + lax.axis_index("gy")) * nz + lax.axis_index("gz")

    def dev(d):
        t = lax.rem(me + d, n)
        return t, {"gx": t // (ny * nz), "gy": lax.rem(t // nz, ny), "gz": lax.rem(t, nz)}

    barrier = pltpu.get_barrier_semaphore()

    def greet(d, c):
        pl.semaphore_signal(barrier, inc=1, device_id=dev(d)[1], device_id_type=MESH)
        return c

    lax.fori_loop(1, n, greet, 0)
    pl.semaphore_wait(barrier, n - 1)

    def copy(d):
        t, target = dev(d)
        return pltpu.make_async_remote_copy(
            src_ref=part.at[t],
            dst_ref=got.at[d],
            send_sem=send.at[d],
            recv_sem=recv.at[d],
            device_id=target,
            device_id_type=MESH,
        )

    def start(d, c):
        copy(d).start()
        return c

    lax.fori_loop(1, n, start, 0)
    out[...] = part[me]

    def take(d, c):
        copy(d).wait()
        out[...] += got[d]
        return c

    lax.fori_loop(1, n, take, 0)
    out[...] = out[...] * scale


def on_device(occupied, virtual, kernel_fields, density_grad):
    nocc, bx, by, lanes = occupied.shape
    nvir = virtual.shape[0]
    devices = lax.axis_size("gx") * lax.axis_size("gy") * lax.axis_size("gz")
    sds = lambda *s: jax.ShapeDtypeStruct(s, F32)
    norb = nocc + nvir
    vmem = pl.BlockSpec(memory_space=pltpu.VMEM)
    plane = bx * by
    flat = lambda a: a.reshape(-1, lanes)
    orb, fld, zed, zfl = pl.pallas_call(
        functools.partial(prep_kernel, plane),
        out_shape=(
            sds(plane, norb, lanes),
            sds(plane, 8, lanes),
            sds(plane, 2, lanes),
            sds(plane, 8, lanes),
        ),
        in_specs=[vmem] * 4,
        out_specs=[vmem] * 4,
        name="prep",
    )(flat(occupied), flat(virtual), flat(kernel_fields), flat(density_grad))
    by_cell = lambda a: a.reshape((bx, by) + a.shape[1:])

    halos = pl.pallas_call(
        halo_kernel,
        out_shape=(
            sds(bx + 8, by + 8, norb, lanes),
            sds(bx + 4, by + 4, 8, lanes),
            sds(2, bx + 4, by + 4, 2, lanes),
            sds(2, bx, by, 8, lanes),
        ),
        in_specs=[vmem] * 4,
        out_specs=[vmem] * 4,
        scratch_shapes=[
            pltpu.SemaphoreType.DMA((26,)),
            pltpu.SemaphoreType.DMA((26,)),
            pltpu.SemaphoreType.DMA((2,)),
        ],
        compiler_params=pltpu.CompilerParams(collective_id=0, has_side_effects=True),
        name="halo",
    )(by_cell(orb), by_cell(fld), by_cell(zed), by_cell(zfl))

    cells = bx * by * lanes
    pairs = nocc * nvir
    wide = lambda *s: pltpu.VMEM(s + (nvir, lanes), F32)
    pot, part = pl.pallas_call(
        functools.partial(main_kernel, (nocc, nvir)),
        grid=(nocc,),
        out_shape=(sds(pairs * bx * by, lanes), sds(pairs, pairs)),
        in_specs=[vmem] * 4,
        out_specs=(
            pl.BlockSpec((nvir * bx * by, lanes), lambda i: (i, 0)),
            pl.BlockSpec((pairs, pairs), lambda i: (0, 0)),
        ),
        scratch_shapes=[
            wide(bx + 8, by + 8),
            pltpu.VMEM((4, bx + 4, by + 4, nocc, lanes), F32),
            wide(4, bx + 4, by + 4),
            wide(1, bx + 4, by + 4),
            wide(bx, by),
            pltpu.VMEM((7, bx, by, 8, lanes), F32),
            pltpu.VMEM((4, 4 * by, 8, lanes), F32),
            pltpu.VMEM((4, 4 * bx, 8, lanes), F32),
            wide(bx + 4, by),
            wide(bx, by + 4),
            wide(1),
            wide(bx, by),
        ]
        + [pltpu.VMEM((pairs, cells), BF16)] * 4,
        compiler_params=pltpu.CompilerParams(
            dimension_semantics=("arbitrary",), vmem_limit_bytes=50 * 1024 * 1024
        ),
        name="response",
    )(*halos)

    rows = pairs // devices
    casida = pl.pallas_call(
        functools.partial(scatter_kernel, 1.0 / (cells * devices)),
        out_shape=sds(rows, pairs),
        in_specs=[vmem],
        out_specs=vmem,
        scratch_shapes=[
            pltpu.VMEM((devices, rows, pairs), F32),
            pltpu.SemaphoreType.DMA((devices,)),
            pltpu.SemaphoreType.DMA((devices,)),
        ],
        compiler_params=pltpu.CompilerParams(collective_id=1, has_side_effects=True),
        name="scatter",
    )(part.reshape(devices, rows, pairs))
    return pot.reshape(pairs, bx, by, lanes), casida


def solution(mesh):
    spec = P(None, "gx", "gy", "gz")
    return jax.shard_map(
        on_device,
        mesh=mesh,
        in_specs=(spec,) * 4,
        out_specs=(spec, P(("gx", "gy", "gz"), None)),
        check_vma=False,
    )
```

time: 119 us -> 89.7 us (0.75)
  Pallas kernels: 95.2 us -> 82.3 us
  local copies, waits for them, and re-layouts: 19.2 us -> 6.41 us
  other arithmetic: 2.44 us -> 0 us
    pallas_call x1, Pallas kernels: 52.6 us -> 39.1 us  [on_device(): pl.pallas_call(functools.partial(main_kernel, (nocc, nvir)), grid=(nocc,)...]
    slice x12 -> x0, local copies, waits for them, and re-layouts: 5.63 us -> none  [the longest x6 3.46 us: slots(): lo = jnp.roll(turned[..., :4], 1, axis=0)]
    unnamed x36 -> x11, local copies, waits for them, and re-layouts: 12 us -> 6.41 us
    another operation x4 -> x0, local copies, waits for them, and re-layouts: 1.39 us -> none  [the longest x2 1.15 us: on_device(): zfl = jnp.tile(ends, (1, 1, 1, lanes // 8))]
    pallas_call x1 -> x2, Pallas kernels: 29.1 us -> 30.2 us  [the longest x1 23.9 us: on_device(): pl.pallas_call(halo_kernel, out_shape=(sds(bx + 8, by + 8, norb, lanes),...]
where the time goes in v2:
time: 89.7 us; the launch traced here: 89.3 us
  Pallas kernels  82.3 us (92%)
  local copies, waits for them, and re-layouts  6.41 us (7%)
    pallas_call x1, Pallas kernels, on_device(): pl.pallas_call(functools.partial(main_kernel, (nocc, nvir)), grid=(nocc,)...  39.1 us
    pallas_call x1, Pallas kernels, on_device(): pl.pallas_call(halo_kernel, out_shape=(sds(bx + 8, by + 8, norb, lanes),...  23.9 us
    pallas_call x1, Pallas kernels, on_device(): pl.pallas_call(functools.partial(scatter_kernel, 1.0 / (cells * devices))...  13 us
    unnamed x11, local copies, waits for them, and re-layouts  6.41 us
    pallas_call x1, Pallas kernels, on_device(): pl.pallas_call(functools.partial(prep_kernel, plane), out_shape=(sds(plan...  6.29 us

profile of v2, /device:TPU:0, one launch (start us, length us, event | category | flops | bytes accessed | tf_op | source)
XLA Modules:
  0.0 89.3 jit_solution(17015443494737174508)
XLA Ops:
  0.6 6.3 %prep.1 = (f32[16,32,128]{2,1,0:T(8,128)}, f32[16,8,128]{2,1,0:T(8,128)}, f32[16,2,128]{2,1,0:T(2,128)}, f32[16,8,128]{2,1,0:T(8,128)}) custom-call(f32[256,128]{1,0:T(8,128)} %bitcast.12, f32[256,128]{1,0:T(8,128)} %bitcast.13, f32[64,128]{1,0:T(8,128)} %bitcast.16, f32[48,128]{1,0:T(8,128)} %bitcast.17), custom_call_target="tpu_custom_call" | custom-call | tf_op jit(solution)/shard_map/prep/pallas_call | solution.py:425
  6.9 23.9 %halo.1 = (f32[12,12,32,128]{3,2,1,0:T(8,128)}, f32[8,8,8,128]{3,2,1,0:T(8,128)}, f32[2,8,8,2,128]{4,3,2,1,0:T(2,128)}, f32[2,4,4,8,128]{4,3,2,1,0:T(8,128)}) custom-call(f32[4,4,32,128]{3,2,1,0:T(8,128)} %bitcast.11, f32[4,4,8,128]{3,2,1,0:T(8,128)} %bitcast.14, f32[4,4,2,128]{3,2,1,0:T(2,128)} %bitcast.18, f32[4,4,8,128]{3,2,1,0:T(8,128)} %bitcast.15), custom_call_target="tpu_custom_call" | custom-call | tf_op jit(solution)/shard_map/halo/pallas_call | solution.py:439
  30.8 0.0 copy-start
  30.8 1.7 %copy-done = f32[12,12,32,128]{3,2,1,0:T(8,128)S(1)} copy-done((f32[12,12,32,128]{3,2,1,0:T(8,128)S(1)}, f32[12,12,32,128]{3,2,1,0:T(8,128)}, u32[]{:S(2)}) %copy-start) | copy-done | bytes 2359320
  32.5 0.0 copy-start.2
  32.5 0.9 %copy-done.2 = f32[8,8,8,128]{3,2,1,0:T(8,128)S(1)} copy-done((f32[8,8,8,128]{3,2,1,0:T(8,128)S(1)}, f32[8,8,8,128]{3,2,1,0:T(8,128)}, u32[]{:S(2)}) %copy-start.2) | copy-done | bytes 262168
  33.4 0.0 copy-start.3
  33.4 0.9 %copy-done.3 = f32[2,8,8,2,128]{4,3,2,1,0:T(2,128)S(1)} copy-done((f32[2,8,8,2,128]{4,3,2,1,0:T(2,128)S(1)}, f32[2,8,8,2,128]{4,3,2,1,0:T(2,128)}, u32[]{:S(2)}) %copy-start.3) | copy-done | bytes 131096
  34.3 0.0 copy-start.4
  34.3 0.9 %copy-done.4 = f32[2,4,4,8,128]{4,3,2,1,0:T(8,128)S(1)} copy-done((f32[2,4,4,8,128]{4,3,2,1,0:T(8,128)S(1)}, f32[2,4,4,8,128]{4,3,2,1,0:T(8,128)}, u32[]{:S(2)}) %copy-start.4) | copy-done | bytes 131096
  35.2 39.1 %response.1 = (f32[4096,128]{1,0:T(8,128)}, f32[256,256]{1,0:T(8,128)S(1)}) custom-call(f32[12,12,32,128]{3,2,1,0:T(8,128)S(1)} %copy-done, f32[8,8,8,128]{3,2,1,0:T(8,128)S(1)} %copy-done.2, f32[2,8,8,2,128]{4,3,2,1,0:T(2,128)S(1)} %copy-done.3, f32[2,4,4,8,128]{4,3,2,1,0:T(8,128)S(1)} %copy-done.4), custom_call_target="tpu_custom_call" | custom-call | tf_op jit(solution)/shard_map/response/pallas_call | solution.py:461
  74.3 0.0 copy-start.1
  74.3 0.7 copy-done.1
  75.0 13.0 %scatter.1 = f32[8,256]{1,0:T(8,128)} custom-call(f32[32,8,256]{2,1,0:T(8,128)} %bitcast.10), custom_call_target="tpu_custom_call" | custom-call | tf_op jit(solution)/shard_map/scatter/pallas_call | solution.py:492
  88.0 1.3 %copy.7 = f32[8,256]{1,0:T(8,128)} copy(f32[8,256]{1,0:T(8,128)} %scatter.1) | data formatting | bytes 16384
Async XLA Ops:
  30.8 1.7 %copy-start = (f32[12,12,32,128]{3,2,1,0:T(8,128)S(1)}, f32[12,12,32,128]{3,2,1,0:T(8,128)}, u32[]{:S(2)}) copy-start(f32[12,12,32,128]{3,2,1,0:T(8,128)} %get-tuple-element.16.wide) | copy-start | bytes 7077892
  32.5 0.9 %copy-start.2 = (f32[8,8,8,128]{3,2,1,0:T(8,128)S(1)}, f32[8,8,8,128]{3,2,1,0:T(8,128)}, u32[]{:S(2)}) copy-start(f32[8,8,8,128]{3,2,1,0:T(8,128)} %get-tuple-element.17.wfld) | copy-start | bytes 786436
  33.4 0.9 %copy-start.3 = (f32[2,8,8,2,128]{4,3,2,1,0:T(2,128)S(1)}, f32[2,8,8,2,128]{4,3,2,1,0:T(2,128)}, u32[]{:S(2)}) copy-start(f32[2,8,8,2,128]{4,3,2,1,0:T(2,128)} %get-tuple-element.18.wz) | copy-start | bytes 393220
  34.3 0.9 %copy-start.4 = (f32[2,4,4,8,128]{4,3,2,1,0:T(8,128)S(1)}, f32[2,4,4,8,128]{4,3,2,1,0:T(8,128)}, u32[]{:S(2)}) copy-start(f32[2,4,4,8,128]{4,3,2,1,0:T(8,128)} %get-tuple-element.19.wg) | copy-start | bytes 393220
  74.3 0.7 copy-start.1

commit v3 on v2

--- a/solution.py
+++ b/solution.py
@@ -17,8 +17,10 @@
     v = jnp.where((lane < 4) | (lane >= lanes - 4), v, 0.0)
     step = 8
     while step < lanes:
-        v = v + pltpu.roll(v, step, 1)
-        step *= 2
+        turns = [pltpu.roll(v, k * step, 1) for k in range(1, 4) if k * step < lanes]
+        for t in turns:
+            v = v + t
+        step *= 4
     return v
 
 
@@ -47,7 +49,7 @@
         zfl[c] = spread(eight, lax.broadcasted_iota(jnp.int32, eight.shape, 1))
         return carry
 
-    lax.fori_loop(0, cells, cell, 0)
+    lax.fori_loop(0, cells, cell, 0, unroll=4)
 
 
 def halo_kernel(orb, fld, zed, zfl, wide, wfld, wz, wg, send, recv, own):
@@ -231,14 +233,14 @@
             prepare(t // by, 2 + lax.rem(t, by))
             return c
 
-        lax.fori_loop(0, (bx + 4) * by, band, 0)
+        lax.fori_loop(0, (bx + 4) * by, band, 0, unroll=4)
 
         def sides(t, c):
             y = lax.rem(t, 4)
             prepare(2 + t // 4, jnp.where(y < 2, y, y + by))
             return c
 
-        lax.fori_loop(0, bx * 4, sides, 0)
+        lax.fori_loop(0, bx * 4, sides, 0, unroll=4)
 
         def flux_at(me, f, s, n):
             g = [f[k:k + 1] for k in range(3)]
@@ -269,7 +271,7 @@
                 C[k, x - 2, y - 2] = jnp.broadcast_to(f[k:k + 1], (8, lanes))
             return carry
 
-        lax.fori_loop(0, bx * by, edges, 0)
+        lax.fori_loop(0, bx * by, edges, 0, unroll=4)
 
         def arm_coefs(arm, at, me, f):
             gm = f[me:me + 1]
@@ -285,14 +287,14 @@
             arm_coefs(A0, t, 0, wfld[jnp.where(x < 2, x, x + bx), 2 + lax.rem(t, by)])
             return c
 
-        lax.fori_loop(0, 4 * by, arm_x, 0)
+        lax.fori_loop(0, 4 * by, arm_x, 0, unroll=4)
 
         def arm_y(t, c):
             y = lax.rem(t, 4)
             arm_coefs(A1, t, 1, wfld[2 + t // 4, jnp.where(y < 2, y, y + by)])
             return c
 
-        lax.fori_loop(0, 4 * bx, arm_y, 0)
+        lax.fori_loop(0, 4 * bx, arm_y, 0, unroll=4)
 
     def rows2(c):
         return jnp.concatenate([c] * (nvir // 8), axis=0)
@@ -368,55 +370,73 @@
         part[...] = dot(nh, ph) + dot(nh, plo) + dot(nl, ph)
 
 
-def scatter_kernel(scale, part, out, got, send, recv):
+def scatter_kernel(scale, part, out, got, acc, got2, send, recv, send2, recv2):
     nx, ny, nz = (lax.axis_size(a) for a in ("gx", "gy", "gz"))
-    n = nx * ny * nz
-    me = (lax.axis_index("gx") * ny + lax.axis_index("gy")) * nz + lax.axis_index("gz")
-
-    def dev(d):
+    x, y, z = (lax.axis_index(a) for a in ("gx", "gy", "gz"))
+    n = nx * nz
+    me = x * nz + z
+
+    def plane(d):
         t = lax.rem(me + d, n)
-        return t, {"gx": t // (ny * nz), "gy": lax.rem(t // nz, ny), "gz": lax.rem(t, nz)}
+        tx, tz = t // nz, lax.rem(t, nz)
+        return tx, tz, {"gx": tx, "gy": y, "gz": tz}
+
+    def column(d):
+        t = lax.rem(y + d, ny)
+        return t, {"gx": x, "gy": t, "gz": z}
 
     barrier = pltpu.get_barrier_semaphore()
-
-    def greet(d, c):
-        pl.semaphore_signal(barrier, inc=1, device_id=dev(d)[1], device_id_type=MESH)
-        return c
-
-    lax.fori_loop(1, n, greet, 0)
-    pl.semaphore_wait(barrier, n - 1)
-
-    def copy(d):
-        t, target = dev(d)
-        return pltpu.make_async_remote_copy(
-            src_ref=part.at[t],
+    for d in range(1, n):
+        pl.semaphore_signal(barrier, inc=1, device_id=plane(d)[2], device_id_type=MESH)
+    for d in range(1, ny):
+        pl.semaphore_signal(barrier, inc=1, device_id=column(d)[1], device_id_type=MESH)
+    pl.semaphore_wait(barrier, n - 1 + ny - 1)
+
+    first = []
+    for d in range(1, n):
+        tx, tz, target = plane(d)
+        c = pltpu.make_async_remote_copy(
+            src_ref=part.at[tx, :, tz],
             dst_ref=got.at[d],
             send_sem=send.at[d],
             recv_sem=recv.at[d],
             device_id=target,
             device_id_type=MESH,
         )
-
-    def start(d, c):
-        copy(d).start()
-        return c
-
-    lax.fori_loop(1, n, start, 0)
-    out[...] = part[me]
-
-    def take(d, c):
-        copy(d).wait()
-        out[...] += got[d]
-        return c
-
-    lax.fori_loop(1, n, take, 0)
-    out[...] = out[...] * scale
+        c.start()
+        first.append(c)
+    total = part[x, :, z]
+    for d, c in enumerate(first):
+        c.wait_recv()
+        total = total + got[d + 1]
+    acc[...] = total
+    second = []
+    for d in range(1, ny):
+        t, target = column(d)
+        c = pltpu.make_async_remote_copy(
+            src_ref=acc.at[t],
+            dst_ref=got2.at[d],
+            send_sem=send2.at[d],
+            recv_sem=recv2.at[d],
+            device_id=target,
+            device_id_type=MESH,
+        )
+        c.start()
+        second.append(c)
+    for c in first:
+        c.wait_send()
+    total = acc[y]
+    for d, c in enumerate(second):
+        c.wait()
+        total = total + got2[d + 1]
+    out[...] = total * scale
 
 
 def on_device(occupied, virtual, kernel_fields, density_grad):
     nocc, bx, by, lanes = occupied.shape
     nvir = virtual.shape[0]
-    devices = lax.axis_size("gx") * lax.axis_size("gy") * lax.axis_size("gz")
+    nx, ny, nz = (lax.axis_size(a) for a in ("gx", "gy", "gz"))
+    devices = nx * ny * nz
     sds = lambda *s: jax.ShapeDtypeStruct(s, F32)
     norb = nocc + nvir
     vmem = pl.BlockSpec(memory_space=pltpu.VMEM)
@@ -432,6 +452,7 @@
         ),
         in_specs=[vmem] * 4,
         out_specs=[vmem] * 4,
+        compiler_params=pltpu.CompilerParams(vmem_limit_bytes=8 * 1024 * 1024),
         name="prep",
     )(flat(occupied), flat(virtual), flat(kernel_fields), flat(density_grad))
     by_cell = lambda a: a.reshape((bx, by) + a.shape[1:])
@@ -444,14 +465,16 @@
             sds(2, bx + 4, by + 4, 2, lanes),
             sds(2, bx, by, 8, lanes),
         ),
-        in_specs=[vmem] * 4,
-        out_specs=[vmem] * 4,
+        in_specs=[pl.BlockSpec(memory_space=pl.ANY)] * 4,
+        out_specs=[pl.BlockSpec(memory_space=pl.ANY)] * 4,
         scratch_shapes=[
             pltpu.SemaphoreType.DMA((26,)),
             pltpu.SemaphoreType.DMA((26,)),
             pltpu.SemaphoreType.DMA((2,)),
         ],
-        compiler_params=pltpu.CompilerParams(collective_id=0, has_side_effects=True),
+        compiler_params=pltpu.CompilerParams(
+            collective_id=0, has_side_effects=True, vmem_limit_bytes=8 * 1024 * 1024
+        ),
         name="halo",
     )(by_cell(orb), by_cell(fld), by_cell(zed), by_cell(zfl))
 
@@ -483,7 +506,7 @@
         ]
         + [pltpu.VMEM((pairs, cells), BF16)] * 4,
         compiler_params=pltpu.CompilerParams(
-            dimension_semantics=("arbitrary",), vmem_limit_bytes=50 * 1024 * 1024
+            dimension_semantics=("arbitrary",), vmem_limit_bytes=28 * 1024 * 1024
         ),
         name="response",
     )(*halos)
@@ -495,13 +518,17 @@
         in_specs=[vmem],
         out_specs=vmem,
         scratch_shapes=[
-            pltpu.VMEM((devices, rows, pairs), F32),
-            pltpu.SemaphoreType.DMA((devices,)),
-            pltpu.SemaphoreType.DMA((devices,)),
+            pltpu.VMEM((nx * nz, ny, rows, pairs), F32),
+            pltpu.VMEM((ny, rows, pairs), F32),
+            pltpu.VMEM((ny, rows, pairs), F32),
+            pltpu.SemaphoreType.DMA((nx * nz,)),
+            pltpu.SemaphoreType.DMA((nx * nz,)),
+            pltpu.SemaphoreType.DMA((ny,)),
+            pltpu.SemaphoreType.DMA((ny,)),
         ],
         compiler_params=pltpu.CompilerParams(collective_id=1, has_side_effects=True),
         name="scatter",
-    )(part.reshape(devices, rows, pairs))
+    )(part.reshape(nx, ny, nz, rows, pairs))
     return pot.reshape(pairs, bx, by, lanes), casida
 
 

time: 89.7 us -> 66.8 us (0.74)
  Pallas kernels: 82.3 us -> 60.5 us
  local copies, waits for them, and re-layouts: 6.41 us -> 5.29 us
    pallas_call x1, Pallas kernels: 39.1 us -> 26.1 us  [on_device(): pl.pallas_call(functools.partial(main_kernel, (nocc, nvir)), grid=(nocc,)...]
    pallas_call x1, Pallas kernels: 6.29 us -> 1 us  [on_device(): pl.pallas_call(functools.partial(prep_kernel, plane), out_shape=(sds(plan...]
    pallas_call x1, Pallas kernels: 23.9 us -> 21.3 us  [on_device(): pl.pallas_call(halo_kernel, out_shape=(sds(bx + 8, by + 8, norb, lanes),...]
    unnamed x11, local copies, waits for them, and re-layouts: 6.41 us -> 5.29 us
    pallas_call x1, Pallas kernels: 13 us -> 12 us  [on_device(): pl.pallas_call(functools.partial(scatter_kernel, 1.0 / (cells * devices))...]
where the time goes in v3:
time: 66.8 us; the launch traced here: 66.4 us
  Pallas kernels  60.5 us (91%)
  local copies, waits for them, and re-layouts  5.29 us (8%)
    pallas_call x1, Pallas kernels, on_device(): pl.pallas_call(functools.partial(main_kernel, (nocc, nvir)), grid=(nocc,)...  26.1 us
    pallas_call x1, Pallas kernels, on_device(): pl.pallas_call(halo_kernel, out_shape=(sds(bx + 8, by + 8, norb, lanes),...  21.3 us
    pallas_call x1, Pallas kernels, on_device(): pl.pallas_call(functools.partial(scatter_kernel, 1.0 / (cells * devices))...  12 us
    unnamed x11, local copies, waits for them, and re-layouts  5.29 us

profile of v3, /device:TPU:0, one launch (start us, length us, event | category | flops | bytes accessed | tf_op | source)
XLA Modules:
  0.0 66.4 jit_solution(2575997745040549596)
XLA Ops:
  0.6 0.0 copy-start.1
  0.6 0.9 %copy-done.1 = f32[16,4,4,128]{3,2,1,0:T(4,128)S(1)} copy-done((f32[16,4,4,128]{3,2,1,0:T(4,128)S(1)}, f32[16,4,4,128]{3,2,1,0:T(4,128)}, u32[]{:S(2)}) %copy-start.1) | copy-done | bytes 131096
  1.5 0.0 copy-start.2
  1.5 0.9 %copy-done.2 = f32[16,4,4,128]{3,2,1,0:T(4,128)S(1)} copy-done((f32[16,4,4,128]{3,2,1,0:T(4,128)S(1)}, f32[16,4,4,128]{3,2,1,0:T(4,128)}, u32[]{:S(2)}) %copy-start.2) | copy-done | bytes 131096
  2.4 0.0 copy-start.3
  2.4 0.8 %copy-done.3 = f32[4,4,4,128]{3,2,1,0:T(4,128)S(1)} copy-done((f32[4,4,4,128]{3,2,1,0:T(4,128)S(1)}, f32[4,4,4,128]{3,2,1,0:T(4,128)}, u32[]{:S(2)}) %copy-start.3) | copy-done | bytes 32792
  3.2 0.0 copy-start.4
  3.2 0.7 %copy-done.4 = f32[3,4,4,128]{3,2,1,0:T(4,128)S(1)} copy-done((f32[3,4,4,128]{3,2,1,0:T(4,128)S(1)}, f32[3,4,4,128]{3,2,1,0:T(4,128)}, u32[]{:S(2)}) %copy-start.4) | copy-done | bytes 24600
  3.9 1.0 %prep.1 = (f32[16,32,128]{2,1,0:T(8,128)S(1)}, f32[16,8,128]{2,1,0:T(8,128)S(1)}, f32[16,2,128]{2,1,0:T(2,128)S(1)}, f32[16,8,128]{2,1,0:T(8,128)S(1)}) custom-call(f32[256,128]{1,0:T(8,128)S(1)} %bitcast.12, f32[256,128]{1,0:T(8,128)S(1)} %bitcast.13, f32[64,128]{1,0:T(8,128)S(1)} %bitcast.16, f32[48,128]{1,0:T(8,128)S(1)} %bitcast.17), custom_call_target="tpu_custom_call" | custom-call | tf_op jit(solution)/shard_map/prep/pallas_call | solution.py:445
  4.9 21.3 %halo.1 = (f32[12,12,32,128]{3,2,1,0:T(8,128)S(1)}, f32[8,8,8,128]{3,2,1,0:T(8,128)S(1)}, f32[2,8,8,2,128]{4,3,2,1,0:T(2,128)S(1)}, f32[2,4,4,8,128]{4,3,2,1,0:T(8,128)S(1)}) custom-call(f32[4,4,32,128]{3,2,1,0:T(8,128)S(1)} %bitcast.10, f32[4,4,8,128]{3,2,1,0:T(8,128)S(1)} %bitcast.14, f32[4,4,2,128]{3,2,1,0:T(2,128)S(1)} %bitcast.18, ...), custom_call_target="tpu_custom_call" | custom-call | tf_op jit(solution)/shard_map/halo/pallas_call | solution.py:460
  26.3 26.1 %response.1 = (f32[4096,128]{1,0:T(8,128)}, f32[256,256]{1,0:T(8,128)S(1)}) custom-call(f32[12,12,32,128]{3,2,1,0:T(8,128)S(1)} %get-tuple-element.16.wide, f32[8,8,8,128]{3,2,1,0:T(8,128)S(1)} %get-tuple-element.17.wfld, f32[2,8,8,2,128]{4,3,2,1,0:T(2,128)S(1)} %get-tuple-element.18.wz, f32[2,4,4,8,128]{4,3,2,1,0:T(8,128)S(1)} %get-tuple-element.19.wg), custom_call_target="tpu_custom_call" | custom-call | tf_op jit(solution)/shard_map/response/pallas_call | solution.py:484
  52.4 0.0 copy-start
  52.4 0.7 %copy-done = f32[256,256]{1,0:T(8,128)} copy-done((f32[256,256]{1,0:T(8,128)}, f32[256,256]{1,0:T(8,128)S(1)}, u32[]{:S(2)}) %copy-start) | copy-done | bytes 262168
  53.1 12.0 %scatter.1 = f32[8,256]{1,0:T(8,128)} custom-call(f32[4,4,2,8,256]{4,3,2,1,0:T(8,128)} %bitcast.11), custom_call_target="tpu_custom_call" | custom-call | tf_op jit(solution)/shard_map/scatter/pallas_call | solution.py:515
  65.1 1.3 %copy.7 = f32[8,256]{1,0:T(8,128)} copy(f32[8,256]{1,0:T(8,128)} %scatter.1) | data formatting | bytes 16384
Async XLA Ops:
  0.6 0.9 %copy-start.1 = (f32[16,4,4,128]{3,2,1,0:T(4,128)S(1)}, f32[16,4,4,128]{3,2,1,0:T(4,128)}, u32[]{:S(2)}) copy-start(f32[16,4,4,128]{3,2,1,0:T(4,128)} %param.4) | copy-start | bytes 393220
  1.5 0.9 %copy-start.2 = (f32[16,4,4,128]{3,2,1,0:T(4,128)S(1)}, f32[16,4,4,128]{3,2,1,0:T(4,128)}, u32[]{:S(2)}) copy-start(f32[16,4,4,128]{3,2,1,0:T(4,128)} %param.5) | copy-start | bytes 393220
  2.4 0.8 %copy-start.3 = (f32[4,4,4,128]{3,2,1,0:T(4,128)S(1)}, f32[4,4,4,128]{3,2,1,0:T(4,128)}, u32[]{:S(2)}) copy-start(f32[4,4,4,128]{3,2,1,0:T(4,128)} %param.6) | copy-start | bytes 98308
  3.2 0.7 %copy-start.4 = (f32[3,4,4,128]{3,2,1,0:T(4,128)S(1)}, f32[3,4,4,128]{3,2,1,0:T(4,128)}, u32[]{:S(2)}) copy-start(f32[3,4,4,128]{3,2,1,0:T(4,128)} %param.7) | copy-start | bytes 73732
  52.4 0.7 %copy-start = (f32[256,256]{1,0:T(8,128)}, f32[256,256]{1,0:T(8,128)S(1)}, u32[]{:S(2)}) copy-start(f32[256,256]{1,0:T(8,128)S(1)} %get-tuple-element.21) | copy-start | bytes 786436
